TPU v7x, 32 devices: a whole 2x2x4 slice. The times are simulated.
32 devices in a mesh: rows: 32 (over z, y, x, core).
Axes of the slice: x: 2, y: 2, z: 4, core: 2. Of those that a mesh axis runs over, the one named last changes fastest.
Arguments:
- events: float32 [4, 32, 262144], P(None, None, 'rows'), may hold values from -8 to 8
- keep_indicator: int32 [4, 262144], P(None, 'rows'), may hold values from 0 to 1, as said below
Outputs:
- lagging_mean: float32 [4, 32, 262144], P(None, None, 'rows')
- deviation: float32 [4, 32, 262144], P(None, None, 'rows')
Inputs may be any that keep to these rules, and one draw needn't show every extreme that they name: `keep_indicator`: in each table, each of the 32 aligned blocks of 8192 rows holds at least 4096 survivors, and some block holds exactly 4096.
All inputs are finite; a program needn't handle non-finite values.
Results may differ from a plain program's by a relative error of at most 0.0003.
Values sent between devices are 32-bit elements; how exact they have to be, the bound alone decides.
A program may use at most 128 MiB of HBM per device.

v0:
```python
import functools

import jax
import jax.numpy as jnp
from jax import lax
from jax.experimental import pallas as pl
from jax.experimental.pallas import tpu as pltpu
from jax.sharding import PartitionSpec as P

SPAN = 4096
LANES = 128
GROUP = 8
F32, BF16, I32 = jnp.float32, jnp.bfloat16, jnp.int32


def iota(shape, axis):
    return lax.broadcasted_iota(I32, shape, axis)


def lane_gather(values, index):
    return jnp.take_along_axis(values, index, axis=1, mode="promise_in_bounds")


def index_kernel(tiles, keep_ref, rank_ref, slot_ref, scalars_ref, flags):
    streams = keep_ref.shape[0]
    rows = streams * tiles
    for s in range(streams):
        for t in range(tiles):
            flags[s * tiles + t : s * tiles + t + 1, :] = keep_ref[s : s + 1, t * LANES : (t + 1) * LANES]
    kept = flags[...].astype(F32).astype(BF16)
    square = (LANES, LANES)
    upper = (iota(square, 0) <= iota(square, 1)).astype(F32).astype(BF16)
    ones = jnp.ones(square, BF16)
    within = jnp.dot(kept, upper, preferred_element_type=F32)
    counts = jnp.dot(kept, ones, preferred_element_type=F32).astype(BF16)
    grid = (rows, rows)
    same = (iota(grid, 0) // tiles) == (iota(grid, 1) // tiles)
    below = (same & (iota(grid, 1) < iota(grid, 0))).astype(F32).astype(BF16)
    above = (same & (iota(grid, 0) < iota(grid, 1))).astype(F32).astype(BF16)
    start = jnp.dot(below, counts, preferred_element_type=F32).astype(I32)
    within = within.astype(I32)
    rank_ref[...] = start + within
    lane = iota((rows, LANES), 1)
    wanted = ((lane - start - 1) & (LANES - 1)) + 1
    position = jnp.zeros((rows, LANES), I32)
    step = LANES // 2
    while step:
        seen = lane_gather(within, position + (step - 1))
        position = jnp.where(seen < wanted, position + step, position)
        step //= 2
    slot_ref[...] = position
    contract = (((1,), (1,)), ((), ()))
    first = (iota((8, LANES), 1) == 0).astype(F32).astype(BF16)
    count_row = lax.dot_general(jnp.ones((8, LANES), BF16), kept, contract, preferred_element_type=F32)
    first_row = lax.dot_general(first, kept, contract, preferred_element_type=F32)
    count_row = count_row.astype(BF16)
    start_row = jnp.dot(count_row, above, preferred_element_type=F32)
    total_row = jnp.dot(count_row, same.astype(F32).astype(BF16), preferred_element_type=F32)
    which = iota((8, rows), 0)
    row = jnp.where(which == 0, start_row, jnp.where(which == 1, total_row, start_row + first_row))
    scalars_ref[...] = row.astype(I32)


def pack_kernel(s, tiles, scalars_ref, events_ref, keep_ref, slot_ref, prefix_ref, table_ref, send_ref, total_ref):
    cols = events_ref.shape[1]
    lane = iota((cols, LANES), 1)
    shape = (2 * LANES, 2 * LANES)
    weights = (((iota(shape, 0) & (LANES - 1)) <= iota(shape, 1)).astype(F32)).astype(BF16)
    width = GROUP * LANES

    def group(g, carry):
        total, current = carry
        columns = pl.ds(pl.multiple_of(g * width, width), width)
        values = jnp.where(keep_ref[s : s + 1, columns] != 0, events_ref[0, :, columns], 0.0)
        high = values.astype(BF16)
        low = (values - high.astype(F32)).astype(BF16)
        left = jnp.concatenate([high[:, i * LANES : (i + 1) * LANES] for i in range(GROUP)], axis=0)
        right = jnp.concatenate([low[:, i * LANES : (i + 1) * LANES] for i in range(GROUP)], axis=0)
        sums = jnp.dot(jnp.concatenate([left, right], axis=1), weights, preferred_element_type=F32)
        for i in range(GROUP):
            t = g * GROUP + i
            piece = sums[i * cols : (i + 1) * cols]
            running = piece[:, :LANES] + total
            total = total + piece[:, LANES:]
            prefix_ref[t] = running
            order = jnp.broadcast_to(slot_ref[pl.ds(t, 1), :], (cols, LANES))
            packed = lane_gather(running, order)
            begin = scalars_ref[0, s * tiles + t] + 1
            block = begin // LANES
            merged = jnp.where(lane >= begin - block * LANES, packed, current)
            table_ref[block] = merged
            following = scalars_ref[0, s * tiles + jnp.minimum(t + 1, tiles - 1)] + 1
            current = jnp.where(following // LANES > block, packed, merged)
            table_ref[block + 1] = packed
        return total, current

    zeros = jnp.zeros((cols, LANES), F32)
    total, _ = lax.fori_loop(0, tiles // GROUP, group, (zeros, zeros))
    total_ref[...] = total
    base = scalars_ref[1, s * tiles] - SPAN
    origin = base // LANES
    offset = base - origin * LANES
    turn = (lane + offset) & (LANES - 1)

    def realign(g, carry):
        for i in range(GROUP):
            m = g * GROUP + i
            mixed = jnp.where(lane >= offset, table_ref[origin + m], table_ref[origin + m + 1])
            send_ref[m] = lane_gather(mixed, turn) - total
        return carry

    lax.fori_loop(0, SPAN // LANES // GROUP, realign, 0)


def spread_kernel(s, tiles, held, scalars_ref, earlier_ref, rank_ref, prefix_ref, before_ref, table_ref, tail_ref, *rest):
    mean_ref, deviation_ref, window, inverse, sems = rest[-5:]
    cols = prefix_ref.shape[1]
    back = SPAN // LANES
    copies = [
        pltpu.make_async_copy(tail_ref, window.at[pl.ds(0, back)], sems.at[0]),
        pltpu.make_async_copy(table_ref.at[pl.ds(0, held)], window.at[pl.ds(back, held)], sems.at[1]),
    ]
    for copy in copies:
        copy.start()
    visited = earlier_ref[s] + rank_ref[...].astype(F32)
    inverse[...] = 1.0 / jnp.maximum(visited, 1.0)
    for copy in copies:
        copy.wait()
    lane = iota((cols, LANES), 1)
    before = before_ref[0]

    def group(g, carry):
        for i in range(GROUP):
            t = g * GROUP + i
            begin = scalars_ref[2, s * tiles + t]
            block = begin // LANES
            mixed = jnp.where(lane >= begin - block * LANES, window[block], window[block + 1])
            order = jnp.broadcast_to(rank_ref[pl.ds(t, 1), :] & (LANES - 1), (cols, LANES))
            running = prefix_ref[t]
            mean = (running - lane_gather(mixed, order)) * (1.0 / SPAN)
            columns = pl.ds(pl.multiple_of(t * LANES, LANES), LANES)
            mean_ref[0, :, columns] = mean
            deviation_ref[0, :, columns] = mean - (running + before) * inverse[pl.ds(t, 1), :]
        return carry

    lax.fori_loop(0, tiles // GROUP, group, 0)


def vmem(*shape):
    return pl.BlockSpec(shape, lambda i: (0,) * len(shape))


def per_device(count, events, keep):
    streams, cols, rows = events.shape
    tiles = rows // LANES
    back = SPAN // LANES
    everything = streams * tiles
    held = (rows - SPAN) // LANES + 2
    smem = pl.BlockSpec(memory_space=pltpu.SMEM)
    anywhere = pl.BlockSpec(memory_space=pl.ANY)

    rank, slot, scalars = pl.pallas_call(
        functools.partial(index_kernel, tiles),
        out_shape=(
            jax.ShapeDtypeStruct((everything, LANES), I32),
            jax.ShapeDtypeStruct((everything, LANES), I32),
            jax.ShapeDtypeStruct((8, everything), I32),
        ),
        scratch_shapes=[pltpu.VMEM((everything, LANES), I32)],
        name="index",
    )(keep)

    prefixes, tables, totals, tails = [], [], [], []
    for s in range(streams):
        prefix, table, send, total = pl.pallas_call(
            functools.partial(pack_kernel, s, tiles),
            grid=(1,),
            in_specs=[
                smem,
                pl.BlockSpec((1, cols, rows), lambda i, s=s: (s, 0, 0)),
                vmem(streams, rows),
                pl.BlockSpec((tiles, LANES), lambda i, s=s: (s, 0)),
            ],
            out_specs=[
                vmem(tiles, cols, LANES),
                vmem(tiles + 2, cols, LANES),
                vmem(back, cols, LANES),
                vmem(cols, LANES),
            ],
            out_shape=[
                jax.ShapeDtypeStruct((tiles, cols, LANES), F32),
                jax.ShapeDtypeStruct((tiles + 2, cols, LANES), F32),
                jax.ShapeDtypeStruct((back, cols, LANES), F32),
                jax.ShapeDtypeStruct((cols, LANES), F32),
            ],
            cost_estimate=pl.CostEstimate(flops=10**8, bytes_accessed=8 * 2**20, transcendentals=0),
            name=f"pack{s}",
        )(scalars, events, keep, slot)
        tails.append(lax.ppermute(send, "rows", [(i, i + 1) for i in range(count - 1)]))
        prefixes.append(prefix)
        tables.append(table)
        totals.append(total)

    summary = jnp.concatenate(
        [jnp.stack([total[:, 0] for total in totals]), scalars[1, ::tiles].astype(F32)[:, None]], axis=1
    )
    gathered = lax.all_gather(summary, "rows", axis=0)
    earlier = jnp.arange(count, dtype=I32) < lax.axis_index("rows")
    before = jnp.sum(jnp.where(earlier[:, None, None], gathered, 0.0), axis=0)
    before_totals = jnp.broadcast_to(before[:, :cols, None], (streams, cols, LANES))
    before_counts = before[:, cols]

    outs = ()
    for s in range(streams):
        outs = pl.pallas_call(
            functools.partial(spread_kernel, s, tiles, held),
            grid=(1,),
            in_specs=[
                smem,
                smem,
                pl.BlockSpec((tiles, LANES), lambda i, s=s: (s, 0)),
                vmem(tiles, cols, LANES),
                pl.BlockSpec((1, cols, LANES), lambda i, s=s: (s, 0, 0)),
                anywhere,
                anywhere,
            ]
            + [anywhere] * len(outs),
            out_specs=[pl.BlockSpec((1, cols, rows), lambda i, s=s: (s, 0, 0))] * 2,
            out_shape=[jax.ShapeDtypeStruct(events.shape, F32)] * 2,
            scratch_shapes=[
                pltpu.VMEM((back + held, cols, LANES), F32),
                pltpu.VMEM((tiles, LANES), F32),
                pltpu.SemaphoreType.DMA((2,)),
            ],
            input_output_aliases={7: 0, 8: 1} if outs else {},
            cost_estimate=pl.CostEstimate(flops=10**8, bytes_accessed=8 * 2**20, transcendentals=0),
            name=f"spread{s}",
        )(scalars, before_counts, rank, prefixes[s], before_totals, tables[s], tails[s], *outs)
    return tuple(outs)


def solution(mesh):
    return jax.shard_map(
        functools.partial(per_device, mesh.shape["rows"]),
        mesh=mesh,
        in_specs=(P(None, None, "rows"), P(None, "rows")),
        out_specs=(P(None, None, "rows"), P(None, None, "rows")),
        check_vma=False,
    )
```

profile of v0, /device:TPU:0, one launch (start us, length us, event | category | flops | bytes accessed | tf_op | source)
XLA Modules:
  0.0 102.7 jit_solution(17901362862202710544)
XLA Ops:
  0.6 2.5 %index.1 = (s32[256,128]{1,0:T(8,128)}, s32[256,128]{1,0:T(8,128)}, s32[8,256]{1,0:T(8,128)}) custom-call(s32[4,8192]{1,0:T(4,128)} %keep_ref.9), custom_call_target="tpu_custom_call" | custom-call | tf_op jit(solution)/shard_map/index/pallas_call | solution.py:162
  3.2 5.6 %pack3.1 = (f32[64,32,128]{2,1,0:T(8,128)}, f32[66,32,128]{2,1,0:T(8,128)}, f32[32,32,128]{2,1,0:T(8,128)}, f32[32,128]{1,0:T(8,128)}) custom-call(s32[8,256]{1,0:T(8,128)} %get-tuple-element.27.scalars_ref, f32[4,32,8192]{2,1,0:T(8,128)} %events_ref.7, s32[4,8192]{1,0:T(4,128)} %keep_ref.9, s32[256,128]{1,0:T(8,128)} %get-tuple-element.28.slot_ref), custom_call_target="tpu_custom_call" | custom-call | flops 100000000 | bytes 8388608 | tf_op jit(solution)/shard_map/pack3/pallas_call | solution.py:175
  8.8 2.4 %collective-permute-start = (f32[32,32,128]{2,1,0:T(8,128)}, f32[32,32,128]{2,1,0:T(8,128)S(1)}, u32[]{:S(2)}, u32[]{:S(2)}) collective-permute-start(f32[32,32,128]{2,1,0:T(8,128)} %get-tuple-element.36), channel_id=1, source_target_pairs={{0,1},{1,2},{2,3},{3,4},{4,5},{5,6},{6,7},{7,8},{8,9},{9,10},{10,1... | collective-permute-start | bytes 1572872 | tf_op jit(solution)/shard_map/ppermute | solution.py:199
  11.2 5.6 %pack2.1 = (f32[64,32,128]{2,1,0:T(8,128)}, f32[66,32,128]{2,1,0:T(8,128)}, f32[32,32,128]{2,1,0:T(8,128)}, f32[32,128]{1,0:T(8,128)}) custom-call(s32[8,256]{1,0:T(8,128)} %get-tuple-element.27.scalars_ref, f32[4,32,8192]{2,1,0:T(8,128)} %events_ref.7, s32[4,8192]{1,0:T(4,128)} %keep_ref.9, s32[256,128]{1,0:T(8,128)} %get-tuple-element.28.slot_ref), custom_call_target="tpu_custom_call" | custom-call | flops 100000000 | bytes 8388608 | tf_op jit(solution)/shard_map/pack2/pallas_call | solution.py:175
  16.8 4.6 %collective-permute-start.1 = (f32[32,32,128]{2,1,0:T(8,128)}, f32[32,32,128]{2,1,0:T(8,128)S(1)}, u32[]{:S(2)}, u32[]{:S(2)}) collective-permute-start(f32[32,32,128]{2,1,0:T(8,128)} %get-tuple-element.39), channel_id=1, source_target_pairs={{0,1},{1,2},{2,3},{3,4},{4,5},{5,6},{6,7},{7,8},{8,9},{9,10},{10,1... | collective-permute-start | bytes 1572872 | tf_op jit(solution)/shard_map/ppermute | solution.py:199
  21.5 5.6 %pack1.1 = (f32[64,32,128]{2,1,0:T(8,128)}, f32[66,32,128]{2,1,0:T(8,128)}, f32[32,32,128]{2,1,0:T(8,128)}, f32[32,128]{1,0:T(8,128)}) custom-call(s32[8,256]{1,0:T(8,128)} %get-tuple-element.27.scalars_ref, f32[4,32,8192]{2,1,0:T(8,128)} %events_ref.7, s32[4,8192]{1,0:T(4,128)} %keep_ref.9, s32[256,128]{1,0:T(8,128)} %get-tuple-element.28.slot_ref), custom_call_target="tpu_custom_call" | custom-call | flops 100000000 | bytes 8388608 | tf_op jit(solution)/shard_map/pack1/pallas_call | solution.py:175
  27.0 2.0 %collective-permute-start.2 = (f32[32,32,128]{2,1,0:T(8,128)}, f32[32,32,128]{2,1,0:T(8,128)S(1)}, u32[]{:S(2)}, u32[]{:S(2)}) collective-permute-start(f32[32,32,128]{2,1,0:T(8,128)} %get-tuple-element.42), channel_id=1, source_target_pairs={{0,1},{1,2},{2,3},{3,4},{4,5},{5,6},{6,7},{7,8},{8,9},{9,10},{10,1... | collective-permute-start | bytes 1572872 | tf_op jit(solution)/shard_map/ppermute | solution.py:199
  29.1 5.6 %pack0.1 = (f32[64,32,128]{2,1,0:T(8,128)}, f32[66,32,128]{2,1,0:T(8,128)}, f32[32,32,128]{2,1,0:T(8,128)}, f32[32,128]{1,0:T(8,128)}) custom-call(s32[8,256]{1,0:T(8,128)} %get-tuple-element.27.scalars_ref, f32[4,32,8192]{2,1,0:T(8,128)} %events_ref.7, s32[4,8192]{1,0:T(4,128)} %keep_ref.9, s32[256,128]{1,0:T(8,128)} %get-tuple-element.28.slot_ref), custom_call_target="tpu_custom_call" | custom-call | flops 100000000 | bytes 8388608 | tf_op jit(solution)/shard_map/pack0/pallas_call | solution.py:175
  34.7 3.5 %collective-permute-start.3 = (f32[32,32,128]{2,1,0:T(8,128)}, f32[32,32,128]{2,1,0:T(8,128)S(1)}, u32[]{:S(2)}, u32[]{:S(2)}) collective-permute-start(f32[32,32,128]{2,1,0:T(8,128)} %get-tuple-element.45), channel_id=1, source_target_pairs={{0,1},{1,2},{2,3},{3,4},{4,5},{5,6},{6,7},{7,8},{8,9},{9,10},{10,1... | collective-permute-start | bytes 1572872 | tf_op jit(solution)/shard_map/ppermute | solution.py:199
  38.1 0.8 slice.25
  38.9 0.1 slice_reduce_fusion
  39.1 0.1 slice_reduce_fusion.1
  39.2 0.1 slice_reduce_fusion.2
  39.3 0.8 slice_reduce_fusion.3
  40.1 0.1 copy.15
  40.2 0.1 maximum_bitcast_fusion
  40.3 38.8 %all-gather.1 = f32[32,4,33]{2,1,0:T(4,128)S(1)} all-gather(f32[1,4,33]{2,1,0:T(4,128)S(1)} %maximum_bitcast_fusion), channel_id=2, replica_groups=mesh['rows'=32] {'rows'}, dimensions={0}, use_global_device_ids=true | all-gather | bytes 17424 | tf_op jit(solution)/shard_map/all_gather | solution.py:207
  79.1 0.1 select_reduce_fusion
  79.3 0.8 slice_reduce_fusion.4.earlier_ref
  80.0 0.0 collective-permute-done.3.tail_ref
  80.0 0.8 broadcast_in_dim.22.before_ref
  80.8 0.0 copy-done.3
  80.8 4.8 %spread0.1 = (f32[4,32,8192]{2,1,0:T(8,128)}, f32[4,32,8192]{2,1,0:T(8,128)}) custom-call(s32[8,256]{1,0:T(8,128)} %get-tuple-element.27.scalars_ref, f32[4]{0:T(128)} %slice_reduce_fusion.4.earlier_ref, s32[256,128]{1,0:T(8,128)} %get-tuple-element.33.rank_ref, f32[64,32,128]{2,1,0:T(8,128)} %get-tuple-element.43.prefix_ref, ...), custom_call_target="tpu_custom_call" | custom-call | flops 100000000 | bytes 8388608 | tf_op jit(solution)/shard_map/spread0/pallas_call | solution.py:215
  85.7 0.0 collective-permute-done.2.tail_ref
  85.7 0.8 copy-done.2
  86.5 4.9 %spread1.1 = (f32[4,32,8192]{2,1,0:T(8,128)}, f32[4,32,8192]{2,1,0:T(8,128)}) custom-call(s32[8,256]{1,0:T(8,128)} %get-tuple-element.27.scalars_ref, f32[4]{0:T(128)} %slice_reduce_fusion.4.earlier_ref, s32[256,128]{1,0:T(8,128)} %get-tuple-element.33.rank_ref, ...), custom_call_target="tpu_custom_call", output_to_operand_aliasing={{0}: (7, {}), {1}: (8, {})} | custom-call | flops 100000000 | bytes 8388608 | tf_op jit(solution)/shard_map/spread1/pallas_call | solution.py:215
  91.3 0.0 collective-permute-done.1.tail_ref
  91.4 0.8 copy-done.1
  92.2 4.9 %spread2.1 = (f32[4,32,8192]{2,1,0:T(8,128)}, f32[4,32,8192]{2,1,0:T(8,128)}) custom-call(s32[8,256]{1,0:T(8,128)} %get-tuple-element.27.scalars_ref, f32[4]{0:T(128)} %slice_reduce_fusion.4.earlier_ref, s32[256,128]{1,0:T(8,128)} %get-tuple-element.33.rank_ref, ...), custom_call_target="tpu_custom_call", output_to_operand_aliasing={{0}: (7, {}), {1}: (8, {})} | custom-call | flops 100000000 | bytes 8388608 | tf_op jit(solution)/shard_map/spread2/pallas_call | solution.py:215
  97.0 0.0 collective-permute-done.tail_ref
  97.1 0.8 copy-done
  97.8 4.9 %spread3.1 = (f32[4,32,8192]{2,1,0:T(8,128)}, f32[4,32,8192]{2,1,0:T(8,128)}) custom-call(s32[8,256]{1,0:T(8,128)} %get-tuple-element.27.scalars_ref, f32[4]{0:T(128)} %slice_reduce_fusion.4.earlier_ref, s32[256,128]{1,0:T(8,128)} %get-tuple-element.33.rank_ref, ...), custom_call_target="tpu_custom_call", output_to_operand_aliasing={{0}: (7, {}), {1}: (8, {})} | custom-call | flops 100000000 | bytes 8388608 | tf_op jit(solution)/shard_map/spread3/pallas_call | solution.py:215
  (12 shorter events, 0.0 us)
Async XLA Ops:
  8.8 88.2 %collective-permute-start = (f32[32,32,128]{2,1,0:T(8,128)}, f32[32,32,128]{2,1,0:T(8,128)S(1)}, u32[]{:S(2)}, u32[]{:S(2)}) collective-permute-start(f32[32,32,128]{2,1,0:T(8,128)} %get-tuple-element.36), channel_id=1, source_target_pairs={{0,1},{1,2},{2,3},{3,4},{4,5},{5,6},{6,7},{7,8},{8,9},{9,10},{10,1... | collective-permute-start | bytes 1572872 | tf_op jit(solution)/shard_map/ppermute | solution.py:199
  16.8 22.1 %copy-start.4 = (f32[32,128]{1,0:T(8,128)S(1)}, f32[32,128]{1,0:T(8,128)}, u32[]{:S(2)}) copy-start(f32[32,128]{1,0:T(8,128)} %get-tuple-element.32) | copy-start | bytes 49156
  16.8 22.2 %copy-start.5 = (f32[32,128]{1,0:T(8,128)S(1)}, f32[32,128]{1,0:T(8,128)}, u32[]{:S(2)}) copy-start(f32[32,128]{1,0:T(8,128)} %get-tuple-element.31) | copy-start | bytes 49156
  16.8 74.5 %collective-permute-start.1 = (f32[32,32,128]{2,1,0:T(8,128)}, f32[32,32,128]{2,1,0:T(8,128)S(1)}, u32[]{:S(2)}, u32[]{:S(2)}) collective-permute-start(f32[32,32,128]{2,1,0:T(8,128)} %get-tuple-element.39), channel_id=1, source_target_pairs={{0,1},{1,2},{2,3},{3,4},{4,5},{5,6},{6,7},{7,8},{8,9},{9,10},{10,1... | collective-permute-start | bytes 1572872 | tf_op jit(solution)/shard_map/ppermute | solution.py:199
  27.0 12.1 %copy-start.6 = (f32[32,128]{1,0:T(8,128)S(1)}, f32[32,128]{1,0:T(8,128)}, u32[]{:S(2)}) copy-start(f32[32,128]{1,0:T(8,128)} %get-tuple-element.30) | copy-start | bytes 49156
  27.0 58.6 %collective-permute-start.2 = (f32[32,32,128]{2,1,0:T(8,128)}, f32[32,32,128]{2,1,0:T(8,128)S(1)}, u32[]{:S(2)}, u32[]{:S(2)}) collective-permute-start(f32[32,32,128]{2,1,0:T(8,128)} %get-tuple-element.42), channel_id=1, source_target_pairs={{0,1},{1,2},{2,3},{3,4},{4,5},{5,6},{6,7},{7,8},{8,9},{9,10},{10,1... | collective-permute-start | bytes 1572872 | tf_op jit(solution)/shard_map/ppermute | solution.py:199
  34.7 45.4 %collective-permute-start.3 = (f32[32,32,128]{2,1,0:T(8,128)}, f32[32,32,128]{2,1,0:T(8,128)S(1)}, u32[]{:S(2)}, u32[]{:S(2)}) collective-permute-start(f32[32,32,128]{2,1,0:T(8,128)} %get-tuple-element.45), channel_id=1, source_target_pairs={{0,1},{1,2},{2,3},{3,4},{4,5},{5,6},{6,7},{7,8},{8,9},{9,10},{10,1... | collective-permute-start | bytes 1572872 | tf_op jit(solution)/shard_map/ppermute | solution.py:199
  80.0 0.8 copy-start.3
  85.7 0.8 copy-start.2
  91.3 0.8 copy-start.1
  97.0 0.8 copy-start
where the time goes:
time: 103 us
  Pallas kernels  44.3 us (43%)
  blocking collectives  38.8 us (38%)
  starting transfers between devices  12.6 us (12%)
  local copies, waits for them, and re-layouts  6 us (6%)
    all_gather x1, blocking collectives, per_device(): gathered = lax.all_gather(summary, 'rows', axis=0)  38.8 us
    pallas_call x4, Pallas kernels, per_device(): pl.pallas_call(functools.partial(pack_kernel, s, tiles), grid=(1,), in_sp...  22.4 us
    pallas_call x4, Pallas kernels, per_device(): pl.pallas_call(functools.partial(spread_kernel, s, tiles, held), grid=(1,...  19.4 us
    ppermute x4, starting transfers between devices, per_device(): lax.ppermute(send, 'rows', [(i, i + 1) for i in range(count - 1)])  12.6 us
    pallas_call x1, Pallas kernels, per_device(): pl.pallas_call(functools.partial(index_kernel, tiles), out_shape=(jax.Sha...  2.54 us
    unnamed x14, local copies, waits for them, and re-layouts  2.42 us
  transfers between devices with their start and end apart: 4, of which 0 were waited for; matrix products, arithmetic and copies ran while one was open for 4% of the time, Pallas kernels for 30%

commit v1 on v0

v1 whole, which is shorter than its diff:
```python
import functools

import jax
import jax.numpy as jnp
from jax import lax
from jax.experimental import pallas as pl
from jax.experimental.pallas import tpu as pltpu
from jax.sharding import PartitionSpec as P

SPAN = 4096
LANES = 128
GROUP = 16
GRANT = 14 * 2**20
MESH = pl.DeviceIdType.MESH
F32, BF16, I32 = jnp.float32, jnp.bfloat16, jnp.int32


def iota(shape, axis):
    return lax.broadcasted_iota(I32, shape, axis)


def lane_gather(values, index):
    return jnp.take_along_axis(values, index, axis=1, mode="promise_in_bounds")


def index_kernel(tiles, keep_ref, rank_ref, slot_ref, scalars_ref, flags):
    streams = keep_ref.shape[0]
    rows = streams * tiles
    for s in range(streams):
        for t in range(tiles):
            flags[s * tiles + t : s * tiles + t + 1, :] = keep_ref[s : s + 1, t * LANES : (t + 1) * LANES]
    kept = flags[...].astype(F32).astype(BF16)
    square = (LANES, LANES)
    upper = (iota(square, 0) <= iota(square, 1)).astype(F32).astype(BF16)
    ones = jnp.ones(square, BF16)
    within = jnp.dot(kept, upper, preferred_element_type=F32)
    counts = jnp.dot(kept, ones, preferred_element_type=F32).astype(BF16)
    grid = (rows, rows)
    same = (iota(grid, 0) // tiles) == (iota(grid, 1) // tiles)
    below = (same & (iota(grid, 1) < iota(grid, 0))).astype(F32).astype(BF16)
    above = (same & (iota(grid, 0) < iota(grid, 1))).astype(F32).astype(BF16)
    start = jnp.dot(below, counts, preferred_element_type=F32).astype(I32)
    within = within.astype(I32)
    rank_ref[...] = start + within
    lane = iota((rows, LANES), 1)
    wanted = ((lane - start - 1) & (LANES - 1)) + 1
    position = jnp.zeros((rows, LANES), I32)
    step = LANES // 2
    while step:
        seen = lane_gather(within, position + (step - 1))
        position = jnp.where(seen < wanted, position + step, position)
        step //= 2
    slot_ref[...] = position
    contract = (((1,), (1,)), ((), ()))
    first = (iota((8, LANES), 1) == 0).astype(F32).astype(BF16)
    count_row = lax.dot_general(jnp.ones((8, LANES), BF16), kept, contract, preferred_element_type=F32)
    first_row = lax.dot_general(first, kept, contract, preferred_element_type=F32)
    count_row = count_row.astype(BF16)
    start_row = jnp.dot(count_row, above, preferred_element_type=F32)
    total_row = jnp.dot(count_row, same.astype(F32).astype(BF16), preferred_element_type=F32)
    which = iota((8, rows), 0)
    row = jnp.where(which == 0, start_row, jnp.where(which == 1, total_row, start_row + first_row))
    scalars_ref[...] = row.astype(I32)


def pack_kernel(s, tiles, group, scalars_ref, events_ref, keep_ref, slot_ref, *rest):
    prefix_ref, table_out, send_ref, total_ref, table_ref, current_ref, sem = rest[-7:]
    cols = events_ref.shape[1]
    held = table_out.shape[0]
    g = pl.program_id(0)
    lane = iota((cols, LANES), 1)
    shape = (2 * LANES, 2 * LANES)
    weights = (((iota(shape, 0) & (LANES - 1)) <= iota(shape, 1)).astype(F32)).astype(BF16)

    @pl.when(g == 0)
    def _():
        total_ref[...] = jnp.zeros((cols, LANES), F32)
        current_ref[...] = jnp.zeros((cols, LANES), F32)

    values = jnp.where(keep_ref[s : s + 1, :] != 0, events_ref[0], 0.0)
    high = values.astype(BF16)
    low = (values - high.astype(F32)).astype(BF16)
    left = jnp.concatenate([high[:, i * LANES : (i + 1) * LANES] for i in range(group)], axis=0)
    right = jnp.concatenate([low[:, i * LANES : (i + 1) * LANES] for i in range(group)], axis=0)
    sums = jnp.dot(jnp.concatenate([left, right], axis=1), weights, preferred_element_type=F32)
    total = total_ref[...]
    current = current_ref[...]
    for i in range(group):
        t = g * group + i
        piece = sums[i * cols : (i + 1) * cols]
        running = piece[:, :LANES] + total
        total = total + piece[:, LANES:]
        prefix_ref[i] = running
        order = jnp.broadcast_to(slot_ref[pl.ds(t, 1), :], (cols, LANES))
        packed = lane_gather(running, order)
        begin = scalars_ref[0, s * tiles + t] + 1
        block = begin // LANES
        merged = jnp.where(lane >= begin - block * LANES, packed, current)
        table_ref[block] = merged
        following = scalars_ref[0, s * tiles + jnp.minimum(t + 1, tiles - 1)] + 1
        current = jnp.where(following // LANES > block, packed, merged)
        if i == group - 1:
            table_ref[block + 1] = packed
    total_ref[...] = total
    current_ref[...] = current

    @pl.when(g == pl.num_programs(0) - 1)
    def _():
        copy = pltpu.make_async_copy(table_ref.at[pl.ds(0, held)], table_out, sem)
        copy.start()
        base = scalars_ref[1, s * tiles] - SPAN
        origin = base // LANES
        offset = base - origin * LANES
        turn = (lane + offset) & (LANES - 1)
        for m in range(SPAN // LANES):
            mixed = jnp.where(lane >= offset, table_ref[origin + m], table_ref[origin + m + 1])
            send_ref[m] = lane_gather(mixed, turn) - total
        copy.wait()


def exchange_kernel(count, streams, tiles, scalars_ref, *rest):
    total_refs, (before_ref, mine, slots, send_sems, recv_sems) = rest[:streams], rest[streams:]
    me = lax.axis_index("rows")
    barrier = pltpu.get_barrier_semaphore()

    def greet(j, carry):
        @pl.when(j < me)
        def _():
            pl.semaphore_signal(barrier, inc=1, device_id=(j,), device_id_type=MESH)

        return carry

    lax.fori_loop(0, count, greet, 0)
    width = mine.shape[1]
    cols = width // streams
    stacked = jnp.concatenate([ref[...] for ref in total_refs], axis=0)
    spread = jnp.full((8, LANES), 1.0 / LANES, F32)
    sums = lax.dot_general(
        spread, stacked, (((1,), (1,)), ((), ())), precision=lax.Precision.HIGHEST, preferred_element_type=F32
    )
    row, column = iota((8, width), 0), iota((8, width), 1)
    counts = jnp.zeros((8, width), F32)
    for s in range(streams):
        counts = jnp.where(column // cols == s, scalars_ref[1, s * tiles].astype(F32), counts)
    mine[...] = jnp.where(row == 0, sums, counts)
    before_ref[...] = jnp.zeros((8, width), F32)

    @pl.when(me < count - 1)
    def _():
        pl.semaphore_wait(barrier, count - 1 - me)

    def copy_to(j):
        return pltpu.make_async_remote_copy(
            src_ref=mine,
            dst_ref=slots.at[me],
            send_sem=send_sems.at[j],
            recv_sem=recv_sems.at[me],
            device_id=(j,),
            device_id_type=MESH,
        )

    def send(j, carry):
        @pl.when(j > me)
        def _():
            copy_to(j).start()

        return carry

    def receive(j, carry):
        @pl.when(j < me)
        def _():
            pltpu.make_async_remote_copy(
                src_ref=mine,
                dst_ref=slots.at[j],
                send_sem=send_sems.at[j],
                recv_sem=recv_sems.at[j],
                device_id=(j,),
                device_id_type=MESH,
            ).wait_recv()
            before_ref[...] += slots[j]

        return carry

    def finish(j, carry):
        @pl.when(j > me)
        def _():
            copy_to(j).wait_send()

        return carry

    lax.fori_loop(0, count, send, 0)
    lax.fori_loop(0, count, receive, 0)
    lax.fori_loop(0, count, finish, 0)


def spread_kernel(s, tiles, group, held, scalars_ref, before_ref, rank_ref, prefix_ref, table_ref, tail_ref, *rest):
    mean_ref, deviation_ref, window, inverse, offsets, sems = rest[-6:]
    cols = prefix_ref.shape[1]
    back = SPAN // LANES
    g = pl.program_id(0)

    @pl.when(g == 0)
    def _():
        copies = [
            pltpu.make_async_copy(tail_ref, window.at[pl.ds(0, back)], sems.at[0]),
            pltpu.make_async_copy(table_ref, window.at[pl.ds(back, held)], sems.at[1]),
        ]
        for copy in copies:
            copy.start()
        width = before_ref.shape[1]
        shape = (cols, width)
        mine = iota(shape, 1) == iota(shape, 0) + s * cols
        column = jnp.sum(jnp.where(mine, before_ref[0:1, :], 0.0), axis=1, keepdims=True)
        offsets[...] = jnp.broadcast_to(column, (cols, LANES))
        first = iota((1, width), 1) == s * cols
        earlier = jnp.sum(jnp.where(first, before_ref[1:2, :], 0.0), axis=1, keepdims=True)
        inverse[...] = 1.0 / jnp.maximum(earlier + rank_ref[...].astype(F32), 1.0)
        for copy in copies:
            copy.wait()

    lane = iota((cols, LANES), 1)
    before = offsets[...]
    for i in range(group):
        t = g * group + i
        begin = scalars_ref[2, s * tiles + t]
        block = begin // LANES
        mixed = jnp.where(lane >= begin - block * LANES, window[block], window[block + 1])
        order = jnp.broadcast_to(rank_ref[pl.ds(t, 1), :] & (LANES - 1), (cols, LANES))
        running = prefix_ref[i]
        mean = (running - lane_gather(mixed, order)) * (1.0 / SPAN)
        mean_ref[0, :, i * LANES : (i + 1) * LANES] = mean
        deviation_ref[0, :, i * LANES : (i + 1) * LANES] = mean - (running + before) * inverse[pl.ds(t, 1), :]


def whole(*shape):
    return pl.BlockSpec(shape, lambda i: (0,) * len(shape))


def per_device(count, events, keep):
    streams, cols, rows = events.shape
    tiles = rows // LANES
    back = SPAN // LANES
    everything = streams * tiles
    held = (rows - SPAN) // LANES + 2
    group = min(GROUP, tiles)
    steps = tiles // group
    smem = pl.BlockSpec(memory_space=pltpu.SMEM)
    anywhere = pl.BlockSpec(memory_space=pl.ANY)
    cost = pl.CostEstimate(flops=10**8, bytes_accessed=8 * 2**20, transcendentals=0)

    rank, slot, scalars = pl.pallas_call(
        functools.partial(index_kernel, tiles),
        out_shape=(
            jax.ShapeDtypeStruct((everything, LANES), I32),
            jax.ShapeDtypeStruct((everything, LANES), I32),
            jax.ShapeDtypeStruct((8, everything), I32),
        ),
        scratch_shapes=[pltpu.VMEM((everything, LANES), I32)],
        compiler_params=pltpu.CompilerParams(vmem_limit_bytes=GRANT),
        name="index",
    )(keep)

    prefixes, tables, totals, tails = [], [], [], []
    for s in range(streams):
        prefix, table, send, total = pl.pallas_call(
            functools.partial(pack_kernel, s, tiles, group),
            grid=(steps,),
            in_specs=[
                smem,
                pl.BlockSpec((1, cols, group * LANES), lambda i, s=s: (s, 0, i)),
                pl.BlockSpec((streams, group * LANES), lambda i: (0, i)),
                pl.BlockSpec((tiles, LANES), lambda i, s=s: (s, 0)),
            ]
            + [anywhere] * (s > 0),
            out_specs=[
                pl.BlockSpec((group, cols, LANES), lambda i: (i, 0, 0)),
                anywhere,
                whole(back, cols, LANES),
                whole(cols, LANES),
            ],
            out_shape=[
                jax.ShapeDtypeStruct((tiles, cols, LANES), F32),
                jax.ShapeDtypeStruct((held, cols, LANES), F32),
                jax.ShapeDtypeStruct((back, cols, LANES), F32),
                jax.ShapeDtypeStruct((cols, LANES), F32),
            ],
            scratch_shapes=[
                pltpu.VMEM((tiles + 2, cols, LANES), F32),
                pltpu.VMEM((cols, LANES), F32),
                pltpu.SemaphoreType.DMA,
            ],
            cost_estimate=cost,
            compiler_params=pltpu.CompilerParams(vmem_limit_bytes=GRANT),
            name=f"pack{s}",
        )(scalars, events, keep, slot, *totals[-1:])
        tails.append(lax.ppermute(send, "rows", [(i, i + 1) for i in range(count - 1)]))
        prefixes.append(prefix)
        tables.append(table)
        totals.append(total)

    width = streams * cols
    before = pl.pallas_call(
        functools.partial(exchange_kernel, count, streams, tiles),
        in_specs=[smem] + [pl.BlockSpec(memory_space=pltpu.VMEM)] * streams,
        out_specs=pl.BlockSpec(memory_space=pltpu.VMEM),
        out_shape=jax.ShapeDtypeStruct((8, width), F32),
        scratch_shapes=[
            pltpu.VMEM((8, width), F32),
            pltpu.VMEM((count, 8, width), F32),
            pltpu.SemaphoreType.DMA((count,)),
            pltpu.SemaphoreType.DMA((count,)),
        ],
        compiler_params=pltpu.CompilerParams(collective_id=0, has_side_effects=True, vmem_limit_bytes=GRANT),
        name="exchange",
    )(scalars, *totals)

    outs = ()
    for s in range(streams):
        outs = pl.pallas_call(
            functools.partial(spread_kernel, s, tiles, group, held),
            grid=(steps,),
            in_specs=[
                smem,
                whole(8, width),
                pl.BlockSpec((tiles, LANES), lambda i, s=s: (s, 0)),
                pl.BlockSpec((group, cols, LANES), lambda i: (i, 0, 0)),
                anywhere,
                anywhere,
            ]
            + [anywhere] * len(outs),
            out_specs=[pl.BlockSpec((1, cols, group * LANES), lambda i, s=s: (s, 0, i))] * 2,
            out_shape=[jax.ShapeDtypeStruct(events.shape, F32)] * 2,
            scratch_shapes=[
                pltpu.VMEM((back + held, cols, LANES), F32),
                pltpu.VMEM((tiles, LANES), F32),
                pltpu.VMEM((cols, LANES), F32),
                pltpu.SemaphoreType.DMA((2,)),
            ],
            input_output_aliases={6: 0, 7: 1} if outs else {},
            cost_estimate=cost,
            compiler_params=pltpu.CompilerParams(vmem_limit_bytes=GRANT),
            name=f"spread{s}",
        )(scalars, before, rank, prefixes[s], tables[s], tails[s], *outs)
    return tuple(outs)


def solution(mesh):
    return jax.shard_map(
        functools.partial(per_device, mesh.shape["rows"]),
        mesh=mesh,
        in_specs=(P(None, None, "rows"), P(None, "rows")),
        out_specs=(P(None, None, "rows"), P(None, None, "rows")),
        check_vma=False,
    )
```

time: 103 us -> 53.2 us (0.52)
  the two profiles are of different devices: /device:TPU:0 before, /device:TPU:25 now
where the time goes in v1:
time: 53.2 us; the launch traced here: 53 us
  Pallas kernels  38.1 us (72%)
  starting transfers between devices  11 us (21%)
  local copies, waits for them, and re-layouts  3.08 us (6%)
  between operations  0.77 us (1%)
    pallas_call x1, Pallas kernels, per_device(): pl.pallas_call(functools.partial(exchange_kernel, count, streams, tiles),...  13 us
    pallas_call x4, Pallas kernels, per_device(): pl.pallas_call(functools.partial(spread_kernel, s, tiles, group, held), g...  12.6 us
    pallas_call x4, Pallas kernels, per_device(): pl.pallas_call(functools.partial(pack_kernel, s, tiles, group), grid=(ste...  11.4 us
    ppermute x4, starting transfers between devices, per_device(): lax.ppermute(send, 'rows', [(i, i + 1) for i in range(count - 1)])  11 us
    unnamed x4, local copies, waits for them, and re-layouts  3.08 us
  transfers between devices with their start and end apart: 4, of which 0 were waited for; matrix products, arithmetic and copies ran while one was open for 0% of the time, Pallas kernels for 59%

profile of v1, /device:TPU:25, one launch (start us, length us, event | category | flops | bytes accessed | tf_op | source)
XLA Modules:
  0.0 53.0 jit_solution(3941575646896797737)
XLA Ops:
  0.6 0.0 copy-start.1
  0.6 0.9 %copy-done.1 = s32[4,8192]{1,0:T(4,128)S(1)} copy-done((s32[4,8192]{1,0:T(4,128)S(1)}, s32[4,8192]{1,0:T(4,128)}, u32[]{:S(2)}) %copy-start.1) | copy-done | bytes 131096
  1.5 1.0 %index.1 = (s32[256,128]{1,0:T(8,128)S(1)}, s32[256,128]{1,0:T(8,128)S(1)}, s32[8,256]{1,0:T(8,128)S(1)}) custom-call(s32[4,8192]{1,0:T(4,128)S(1)} %copy-done.1), custom_call_target="tpu_custom_call" | custom-call | tf_op jit(solution)/shard_map/index/pallas_call | solution.py:251
  2.5 0.0 copy-start
  2.5 2.2 %copy-done = f32[4,32,8192]{2,1,0:T(8,128)S(1)} copy-done((f32[4,32,8192]{2,1,0:T(8,128)S(1)}, f32[4,32,8192]{2,1,0:T(8,128)}, u32[]{:S(2)}) %copy-start) | copy-done | bytes 4194328
  4.7 2.8 %pack0.1 = (f32[64,32,128]{2,1,0:T(8,128)S(1)}, f32[34,32,128]{2,1,0:T(8,128)S(1)}, f32[32,32,128]{2,1,0:T(8,128)S(1)}, f32[32,128]{1,0:T(8,128)S(1)}) custom-call(s32[8,256]{1,0:T(8,128)S(1)} %get-tuple-element.27.scalars_ref, f32[4,32,8192]{2,1,0:T(8,128)S(1)} %copy-done, s32[4,8192]{1,0:T(4,128)S(1)} %copy-done.1, s32[256,128]{1,0:T(8,128)S(1)} %get-tuple-element.28.slot_ref), custom_call_target="tpu_custom_call" | custom-call | flops 100000000 | bytes 8388608 | tf_op jit(solution)/shard_map/pack0/pallas_call | solution.py:265
  7.5 3.7 %collective-permute-start.3 = (f32[32,32,128]{2,1,0:T(8,128)S(1)}, f32[32,32,128]{2,1,0:T(8,128)S(1)}, u32[]{:S(2)}, u32[]{:S(2)}) collective-permute-start(f32[32,32,128]{2,1,0:T(8,128)S(1)} %get-tuple-element.45), channel_id=1, source_target_pairs={{0,1},{1,2},{2,3},{3,4},{4,5},{5,6},{6,7},{7,8},{8,9},{9,10},{10,1... | collective-permute-start | bytes 1572872 | tf_op jit(solution)/shard_map/ppermute | solution.py:296
  11.2 2.9 %pack1.1 = (f32[64,32,128]{2,1,0:T(8,128)S(1)}, f32[34,32,128]{2,1,0:T(8,128)S(1)}, f32[32,32,128]{2,1,0:T(8,128)S(1)}, f32[32,128]{1,0:T(8,128)S(1)}) custom-call(s32[8,256]{1,0:T(8,128)S(1)} %get-tuple-element.27.scalars_ref, f32[4,32,8192]{2,1,0:T(8,128)S(1)} %copy-done, s32[4,8192]{1,0:T(4,128)S(1)} %copy-done.1, ...), custom_call_target="tpu_custom_call" | custom-call | flops 100000000 | bytes 8388608 | tf_op jit(solution)/shard_map/pack1/pallas_call | solution.py:265
  14.1 1.9 %collective-permute-start.2 = (f32[32,32,128]{2,1,0:T(8,128)S(1)}, f32[32,32,128]{2,1,0:T(8,128)S(1)}, u32[]{:S(2)}, u32[]{:S(2)}) collective-permute-start(f32[32,32,128]{2,1,0:T(8,128)S(1)} %get-tuple-element.42), channel_id=1, source_target_pairs={{0,1},{1,2},{2,3},{3,4},{4,5},{5,6},{6,7},{7,8},{8,9},{9,10},{10,1... | collective-permute-start | bytes 1572872 | tf_op jit(solution)/shard_map/ppermute | solution.py:296
  16.0 2.9 %pack2.1 = (f32[64,32,128]{2,1,0:T(8,128)S(1)}, f32[34,32,128]{2,1,0:T(8,128)S(1)}, f32[32,32,128]{2,1,0:T(8,128)S(1)}, f32[32,128]{1,0:T(8,128)S(1)}) custom-call(s32[8,256]{1,0:T(8,128)S(1)} %get-tuple-element.27.scalars_ref, f32[4,32,8192]{2,1,0:T(8,128)S(1)} %copy-done, s32[4,8192]{1,0:T(4,128)S(1)} %copy-done.1, ...), custom_call_target="tpu_custom_call" | custom-call | flops 100000000 | bytes 8388608 | tf_op jit(solution)/shard_map/pack2/pallas_call | solution.py:265
  18.9 3.5 %collective-permute-start.1 = (f32[32,32,128]{2,1,0:T(8,128)S(1)}, f32[32,32,128]{2,1,0:T(8,128)S(1)}, u32[]{:S(2)}, u32[]{:S(2)}) collective-permute-start(f32[32,32,128]{2,1,0:T(8,128)S(1)} %get-tuple-element.39), channel_id=1, source_target_pairs={{0,1},{1,2},{2,3},{3,4},{4,5},{5,6},{6,7},{7,8},{8,9},{9,10},{10,1... | collective-permute-start | bytes 1572872 | tf_op jit(solution)/shard_map/ppermute | solution.py:296
  22.4 2.9 %pack3.1 = (f32[64,32,128]{2,1,0:T(8,128)S(1)}, f32[34,32,128]{2,1,0:T(8,128)S(1)}, f32[32,32,128]{2,1,0:T(8,128)S(1)}, f32[32,128]{1,0:T(8,128)S(1)}) custom-call(s32[8,256]{1,0:T(8,128)S(1)} %get-tuple-element.27.scalars_ref, f32[4,32,8192]{2,1,0:T(8,128)S(1)} %copy-done, s32[4,8192]{1,0:T(4,128)S(1)} %copy-done.1, ...), custom_call_target="tpu_custom_call" | custom-call | flops 100000000 | bytes 8388608 | tf_op jit(solution)/shard_map/pack3/pallas_call | solution.py:265
  25.3 1.9 %collective-permute-start = (f32[32,32,128]{2,1,0:T(8,128)S(1)}, f32[32,32,128]{2,1,0:T(8,128)S(1)}, u32[]{:S(2)}, u32[]{:S(2)}) collective-permute-start(f32[32,32,128]{2,1,0:T(8,128)S(1)} %get-tuple-element.36), channel_id=1, source_target_pairs={{0,1},{1,2},{2,3},{3,4},{4,5},{5,6},{6,7},{7,8},{8,9},{9,10},{10,1... | collective-permute-start | bytes 1572872 | tf_op jit(solution)/shard_map/ppermute | solution.py:296
  27.2 13.0 %exchange.1.before_ref = f32[8,128]{1,0:T(8,128)S(1)} custom-call(s32[8,256]{1,0:T(8,128)S(1)} %get-tuple-element.27.scalars_ref, f32[32,128]{1,0:T(8,128)S(1)} %get-tuple-element.29.rest_0_, f32[32,128]{1,0:T(8,128)S(1)} %get-tuple-element.30.rest_0_.rest_1_, f32[32,128]{1,0:T(8,128)S(1)} %get-tuple-element.31.rest_0_.rest_2_, ...), custom_call_target="tpu_custom_call" | custom-call | tf_op jit(solution)/shard_map/exchange/pallas_call | solution.py:302
  40.3 0.0 collective-permute-done.3.tail_ref
  40.3 3.2 %spread0.1 = (f32[4,32,8192]{2,1,0:T(8,128)}, f32[4,32,8192]{2,1,0:T(8,128)}) custom-call(s32[8,256]{1,0:T(8,128)S(1)} %get-tuple-element.27.scalars_ref, f32[8,128]{1,0:T(8,128)S(1)} %exchange.1.before_ref, s32[256,128]{1,0:T(8,128)S(1)} %get-tuple-element.33.rank_ref, f32[64,32,128]{2,1,0:T(8,128)S(1)} %get-tuple-element.43.prefix_ref, ...), custom_call_target="tpu_custom_call" | custom-call | flops 100000000 | bytes 8388608 | tf_op jit(solution)/shard_map/spread0/pallas_call | solution.py:319
  43.5 0.0 collective-permute-done.2.tail_ref
  43.5 3.2 %spread1.1 = (f32[4,32,8192]{2,1,0:T(8,128)}, f32[4,32,8192]{2,1,0:T(8,128)}) custom-call(s32[8,256]{1,0:T(8,128)S(1)} %get-tuple-element.27.scalars_ref, f32[8,128]{1,0:T(8,128)S(1)} %exchange.1.before_ref, s32[256,128]{1,0:T(8,128)S(1)} %get-tuple-element.33.rank_ref, ...), custom_call_target="tpu_custom_call", output_to_operand_aliasing={{0}: (6, {}), {1}: (7, {})} | custom-call | flops 100000000 | bytes 8388608 | tf_op jit(solution)/shard_map/spread1/pallas_call | solution.py:319
  46.6 0.0 collective-permute-done.1.tail_ref
  46.6 3.2 %spread2.1 = (f32[4,32,8192]{2,1,0:T(8,128)}, f32[4,32,8192]{2,1,0:T(8,128)}) custom-call(s32[8,256]{1,0:T(8,128)S(1)} %get-tuple-element.27.scalars_ref, f32[8,128]{1,0:T(8,128)S(1)} %exchange.1.before_ref, s32[256,128]{1,0:T(8,128)S(1)} %get-tuple-element.33.rank_ref, ...), custom_call_target="tpu_custom_call", output_to_operand_aliasing={{0}: (6, {}), {1}: (7, {})} | custom-call | flops 100000000 | bytes 8388608 | tf_op jit(solution)/shard_map/spread2/pallas_call | solution.py:319
  49.8 0.0 collective-permute-done.tail_ref
  49.8 3.2 %spread3.1 = (f32[4,32,8192]{2,1,0:T(8,128)}, f32[4,32,8192]{2,1,0:T(8,128)}) custom-call(s32[8,256]{1,0:T(8,128)S(1)} %get-tuple-element.27.scalars_ref, f32[8,128]{1,0:T(8,128)S(1)} %exchange.1.before_ref, s32[256,128]{1,0:T(8,128)S(1)} %get-tuple-element.33.rank_ref, ...), custom_call_target="tpu_custom_call", output_to_operand_aliasing={{0}: (6, {}), {1}: (7, {})} | custom-call | flops 100000000 | bytes 8388608 | tf_op jit(solution)/shard_map/spread3/pallas_call | solution.py:319
Async XLA Ops:
  0.6 0.9 %copy-start.1 = (s32[4,8192]{1,0:T(4,128)S(1)}, s32[4,8192]{1,0:T(4,128)}, u32[]{:S(2)}) copy-start(s32[4,8192]{1,0:T(4,128)} %keep_ref.9) | copy-start | bytes 393220
  2.5 2.2 %copy-start = (f32[4,32,8192]{2,1,0:T(8,128)S(1)}, f32[4,32,8192]{2,1,0:T(8,128)}, u32[]{:S(2)}) copy-start(f32[4,32,8192]{2,1,0:T(8,128)} %events_ref.7) | copy-start | bytes 12582916
  7.5 32.8 %collective-permute-start.3 = (f32[32,32,128]{2,1,0:T(8,128)S(1)}, f32[32,32,128]{2,1,0:T(8,128)S(1)}, u32[]{:S(2)}, u32[]{:S(2)}) collective-permute-start(f32[32,32,128]{2,1,0:T(8,128)S(1)} %get-tuple-element.45), channel_id=1, source_target_pairs={{0,1},{1,2},{2,3},{3,4},{4,5},{5,6},{6,7},{7,8},{8,9},{9,10},{10,1... | collective-permute-start | bytes 1572872 | tf_op jit(solution)/shard_map/ppermute | solution.py:296
  14.1 29.4 %collective-permute-start.2 = (f32[32,32,128]{2,1,0:T(8,128)S(1)}, f32[32,32,128]{2,1,0:T(8,128)S(1)}, u32[]{:S(2)}, u32[]{:S(2)}) collective-permute-start(f32[32,32,128]{2,1,0:T(8,128)S(1)} %get-tuple-element.42), channel_id=1, source_target_pairs={{0,1},{1,2},{2,3},{3,4},{4,5},{5,6},{6,7},{7,8},{8,9},{9,10},{10,1... | collective-permute-start | bytes 1572872 | tf_op jit(solution)/shard_map/ppermute | solution.py:296
  18.9 27.7 %collective-permute-start.1 = (f32[32,32,128]{2,1,0:T(8,128)S(1)}, f32[32,32,128]{2,1,0:T(8,128)S(1)}, u32[]{:S(2)}, u32[]{:S(2)}) collective-permute-start(f32[32,32,128]{2,1,0:T(8,128)S(1)} %get-tuple-element.39), channel_id=1, source_target_pairs={{0,1},{1,2},{2,3},{3,4},{4,5},{5,6},{6,7},{7,8},{8,9},{9,10},{10,1... | collective-permute-start | bytes 1572872 | tf_op jit(solution)/shard_map/ppermute | solution.py:296
  25.3 24.5 %collective-permute-start = (f32[32,32,128]{2,1,0:T(8,128)S(1)}, f32[32,32,128]{2,1,0:T(8,128)S(1)}, u32[]{:S(2)}, u32[]{:S(2)}) collective-permute-start(f32[32,32,128]{2,1,0:T(8,128)S(1)} %get-tuple-element.36), channel_id=1, source_target_pairs={{0,1},{1,2},{2,3},{3,4},{4,5},{5,6},{6,7},{7,8},{8,9},{9,10},{10,1... | collective-permute-start | bytes 1572872 | tf_op jit(solution)/shard_map/ppermute | solution.py:296

commit v2 on v0

v2 whole, which is shorter than its diff:
```python
import functools

import jax
import jax.numpy as jnp
from jax import lax
from jax.experimental import pallas as pl
from jax.experimental.pallas import tpu as pltpu
from jax.sharding import PartitionSpec as P

SPAN = 4096
LANES = 128
GROUP = 16
GRANT = 20 * 2**20
HEAD_GRANT = 57 * 2**20
MESH = pl.DeviceIdType.MESH
F32, BF16, I32 = jnp.float32, jnp.bfloat16, jnp.int32


def iota(shape, axis):
    return lax.broadcasted_iota(I32, shape, axis)


def lane_gather(values, index):
    return jnp.take_along_axis(values, index, axis=1, mode="promise_in_bounds")


def index_kernel(tiles, keep_ref, rank_ref, slot_ref, scalars_ref, flags):
    streams = keep_ref.shape[0]
    rows = streams * tiles
    for s in range(streams):
        for t in range(tiles):
            flags[s * tiles + t : s * tiles + t + 1, :] = keep_ref[s : s + 1, t * LANES : (t + 1) * LANES]
    kept = flags[...].astype(F32).astype(BF16)
    square = (LANES, LANES)
    upper = (iota(square, 0) <= iota(square, 1)).astype(F32).astype(BF16)
    ones = jnp.ones(square, BF16)
    within = jnp.dot(kept, upper, preferred_element_type=F32)
    counts = jnp.dot(kept, ones, preferred_element_type=F32).astype(BF16)
    grid = (rows, rows)
    same = (iota(grid, 0) // tiles) == (iota(grid, 1) // tiles)
    below = (same & (iota(grid, 1) < iota(grid, 0))).astype(F32).astype(BF16)
    above = (same & (iota(grid, 0) < iota(grid, 1))).astype(F32).astype(BF16)
    start = jnp.dot(below, counts, preferred_element_type=F32).astype(I32)
    within = within.astype(I32)
    rank_ref[...] = start + within
    lane = iota((rows, LANES), 1)
    wanted = ((lane - start - 1) & (LANES - 1)) + 1
    position = jnp.zeros((rows, LANES), I32)
    step = LANES // 2
    while step:
        seen = lane_gather(within, position + (step - 1))
        position = jnp.where(seen < wanted, position + step, position)
        step //= 2
    slot_ref[...] = position
    contract = (((1,), (1,)), ((), ()))
    first = (iota((8, LANES), 1) == 0).astype(F32).astype(BF16)
    count_row = lax.dot_general(jnp.ones((8, LANES), BF16), kept, contract, preferred_element_type=F32)
    first_row = lax.dot_general(first, kept, contract, preferred_element_type=F32)
    count_row = count_row.astype(BF16)
    start_row = jnp.dot(count_row, above, preferred_element_type=F32)
    total_row = jnp.dot(count_row, same.astype(F32).astype(BF16), preferred_element_type=F32)
    which = iota((8, rows), 0)
    row = jnp.where(which == 0, start_row, jnp.where(which == 1, total_row, start_row + first_row))
    scalars_ref[...] = row.astype(I32)


def head_kernel(count, tiles, group, scalars_ref, events_ref, keep_ref, prefix_ref, before_ref, *scratch):
    held, mine, slots, load_sems, send_sems, recv_sems = scratch
    streams, cols, rows = held.shape
    width = streams * cols
    me = lax.axis_index("rows")
    barrier = pltpu.get_barrier_semaphore()

    loads = [pltpu.make_async_copy(events_ref.at[s], held.at[s], load_sems.at[s]) for s in range(streams)]
    for load in loads:
        load.start()

    def greet(j, carry):
        @pl.when(j < me)
        def _():
            pl.semaphore_signal(barrier, inc=1, device_id=(j,), device_id_type=MESH)

        return carry

    lax.fori_loop(0, count, greet, 0)
    span = group * LANES

    def masked(s, g):
        columns = pl.ds(pl.multiple_of(g * span, span), span)
        return jnp.where(keep_ref[s : s + 1, columns] != 0, held[s, :, columns], 0.0)

    totals = []
    for s in range(streams):
        loads[s].wait()

        def add(g, total, s=s):
            values = masked(s, g)
            parts = [values[:, i * LANES : (i + 1) * LANES] for i in range(group)]
            while len(parts) > 1:
                parts = [parts[i] + parts[i + 1] for i in range(0, len(parts), 2)]
            return total + parts[0]

        totals.append(lax.fori_loop(0, tiles // group, add, jnp.zeros((cols, LANES), F32)))
    sums = lax.dot_general(
        jnp.ones((8, LANES), F32),
        jnp.concatenate(totals, axis=0),
        (((1,), (1,)), ((), ())),
        precision=lax.Precision.HIGHEST,
        preferred_element_type=F32,
    )
    row, column = iota((8, width), 0), iota((8, width), 1)
    counts = jnp.zeros((8, width), F32)
    for s in range(streams):
        counts = jnp.where(column // cols == s, scalars_ref[1, s * tiles].astype(F32), counts)
    mine[...] = jnp.where(row == 0, sums, counts)
    before_ref[...] = jnp.zeros((8, width), F32)

    @pl.when(me < count - 1)
    def _():
        pl.semaphore_wait(barrier, count - 1 - me)

    def copy(j, sender):
        return pltpu.make_async_remote_copy(
            src_ref=mine,
            dst_ref=slots.at[sender],
            send_sem=send_sems.at[j],
            recv_sem=recv_sems.at[sender],
            device_id=(j,),
            device_id_type=MESH,
        )

    def send(j, carry):
        @pl.when(j > me)
        def _():
            copy(j, me).start()

        return carry

    lax.fori_loop(0, count, send, 0)

    shape = (2 * LANES, 2 * LANES)
    weights = (((iota(shape, 0) & (LANES - 1)) <= iota(shape, 1)).astype(F32)).astype(BF16)
    for s in range(streams):

        def accumulate(g, total, s=s):
            values = masked(s, g)
            high = values.astype(BF16)
            low = (values - high.astype(F32)).astype(BF16)
            left = jnp.concatenate([high[:, i * LANES : (i + 1) * LANES] for i in range(group)], axis=0)
            right = jnp.concatenate([low[:, i * LANES : (i + 1) * LANES] for i in range(group)], axis=0)
            out = jnp.dot(jnp.concatenate([left, right], axis=1), weights, preferred_element_type=F32)
            for i in range(group):
                piece = out[i * cols : (i + 1) * cols]
                prefix_ref[s * tiles + g * group + i] = piece[:, :LANES] + total
                total = total + piece[:, LANES:]
            return total

        lax.fori_loop(0, tiles // group, accumulate, jnp.zeros((cols, LANES), F32))

    def receive(j, carry):
        @pl.when(j < me)
        def _():
            copy(j, j).wait_recv()
            before_ref[...] += slots[j]

        return carry

    def finish(j, carry):
        @pl.when(j > me)
        def _():
            copy(j, me).wait_send()

        return carry

    lax.fori_loop(0, count, receive, 0)
    lax.fori_loop(0, count, finish, 0)


def pack_kernel(s, tiles, scalars_ref, prefix_ref, slot_ref, *rest):
    table_ref, send_ref = rest[-2:]
    cols = prefix_ref.shape[1]
    lane = iota((cols, LANES), 1)
    current = jnp.zeros((cols, LANES), F32)
    for t in range(tiles):
        order = jnp.broadcast_to(slot_ref[s * tiles + t : s * tiles + t + 1, :], (cols, LANES))
        packed = lane_gather(prefix_ref[s * tiles + t], order)
        begin = scalars_ref[0, s * tiles + t] + 1
        block = begin // LANES
        merged = jnp.where(lane >= begin - block * LANES, packed, current)
        table_ref[block] = merged
        if t == tiles - 1:
            table_ref[block + 1] = packed
        else:
            following = (scalars_ref[0, s * tiles + t + 1] + 1) // LANES
            current = jnp.where(following > block, packed, merged)
    last = prefix_ref[(s + 1) * tiles - 1]
    total = lane_gather(last, jnp.full((cols, LANES), LANES - 1, I32))
    base = scalars_ref[1, s * tiles] - SPAN
    origin = base // LANES
    offset = base - origin * LANES
    turn = (lane + offset) & (LANES - 1)
    below = table_ref[origin]
    for m in range(SPAN // LANES):
        above = table_ref[origin + m + 1]
        send_ref[m] = lane_gather(jnp.where(lane >= offset, below, above), turn) - total
        below = above


def spread_kernel(s, tiles, group, scalars_ref, before_ref, rank_ref, prefix_ref, table_ref, tail_ref, *rest):
    mean_ref, deviation_ref, means, deviations, inverse, sems = rest[-6:]
    cols = prefix_ref.shape[1]
    back = SPAN // LANES
    width = before_ref.shape[1]
    mine = iota((cols, width), 1) == iota((cols, width), 0) + s * cols
    column = jnp.sum(jnp.where(mine, before_ref[0:1, :], 0.0), axis=1, keepdims=True)
    before = jnp.broadcast_to(column, (cols, LANES))
    first = iota((1, width), 1) == s * cols
    earlier = jnp.sum(jnp.where(first, before_ref[1:2, :], 0.0), axis=1, keepdims=True)
    ranks = rank_ref[s * tiles : (s + 1) * tiles, :]
    inverse[...] = 1.0 / jnp.maximum(earlier + ranks.astype(F32), 1.0)
    lane = iota((cols, LANES), 1)

    def fetch(block):
        old = tail_ref[jnp.minimum(block, back - 1)]
        new = table_ref[jnp.maximum(block - back, 0)]
        return jnp.where(block < back, old, new)

    copies = []
    for g in range(tiles // group):
        for i in range(group):
            t = g * group + i
            begin = scalars_ref[2, s * tiles + t]
            block = begin // LANES
            mixed = jnp.where(lane >= begin - block * LANES, fetch(block), fetch(block + 1))
            order = jnp.broadcast_to(rank_ref[s * tiles + t : s * tiles + t + 1, :] & (LANES - 1), (cols, LANES))
            running = prefix_ref[s * tiles + t]
            mean = (running - lane_gather(mixed, order)) * (1.0 / SPAN)
            columns = slice(t * LANES, (t + 1) * LANES)
            means[:, columns] = mean
            deviations[:, columns] = mean - (running + before) * inverse[t : t + 1, :]
        part = pl.ds(g * group * LANES, group * LANES)
        for k, (source, target) in enumerate(((means, mean_ref), (deviations, deviation_ref))):
            copy = pltpu.make_async_copy(source.at[:, part], target.at[s, :, part], sems.at[k, g])
            copy.start()
            copies.append(copy)
    for copy in copies:
        copy.wait()


def per_device(count, events, keep):
    streams, cols, rows = events.shape
    tiles = rows // LANES
    back = SPAN // LANES
    everything = streams * tiles
    width = streams * cols
    group = min(GROUP, tiles)
    smem = pl.BlockSpec(memory_space=pltpu.SMEM)
    vmem = pl.BlockSpec(memory_space=pltpu.VMEM)
    anywhere = pl.BlockSpec(memory_space=pl.ANY)
    cost = pl.CostEstimate(flops=10**8, bytes_accessed=8 * 2**20, transcendentals=0)
    params = pltpu.CompilerParams(vmem_limit_bytes=GRANT)

    rank, slot, scalars = pl.pallas_call(
        functools.partial(index_kernel, tiles),
        out_shape=(
            jax.ShapeDtypeStruct((everything, LANES), I32),
            jax.ShapeDtypeStruct((everything, LANES), I32),
            jax.ShapeDtypeStruct((8, everything), I32),
        ),
        scratch_shapes=[pltpu.VMEM((everything, LANES), I32)],
        compiler_params=params,
        name="index",
    )(keep)

    prefix, before = pl.pallas_call(
        functools.partial(head_kernel, count, tiles, group),
        in_specs=[smem, anywhere, vmem],
        out_specs=[vmem, vmem],
        out_shape=[
            jax.ShapeDtypeStruct((everything, cols, LANES), F32),
            jax.ShapeDtypeStruct((8, width), F32),
        ],
        scratch_shapes=[
            pltpu.VMEM((streams, cols, rows), F32),
            pltpu.VMEM((8, width), F32),
            pltpu.VMEM((count, 8, width), F32),
            pltpu.SemaphoreType.DMA((streams,)),
            pltpu.SemaphoreType.DMA((count,)),
            pltpu.SemaphoreType.DMA((count,)),
        ],
        compiler_params=pltpu.CompilerParams(collective_id=0, has_side_effects=True, vmem_limit_bytes=HEAD_GRANT),
        name="head",
    )(scalars, events, keep)

    tables, tails, sent = [], [], []
    for s in range(streams):
        table, send = pl.pallas_call(
            functools.partial(pack_kernel, s, tiles),
            in_specs=[smem, vmem, vmem] + [anywhere] * (s > 0),
            out_specs=[vmem, vmem],
            out_shape=[
                jax.ShapeDtypeStruct((tiles + 2, cols, LANES), F32),
                jax.ShapeDtypeStruct((back, cols, LANES), F32),
            ],
            cost_estimate=cost,
            compiler_params=params,
            name=f"pack{s}",
        )(scalars, prefix, slot, *tables[-1:])
        tails.append(lax.ppermute(send, "rows", [(i, i + 1) for i in range(count - 1)]))
        tables.append(table)

    outs = ()
    for s in range(streams):
        outs = pl.pallas_call(
            functools.partial(spread_kernel, s, tiles, group),
            in_specs=[smem] + [vmem] * 5 + [anywhere] * len(outs),
            out_specs=[anywhere] * 2,
            out_shape=[jax.ShapeDtypeStruct(events.shape, F32)] * 2,
            scratch_shapes=[
                pltpu.VMEM((cols, rows), F32),
                pltpu.VMEM((cols, rows), F32),
                pltpu.VMEM((tiles, LANES), F32),
                pltpu.SemaphoreType.DMA((2, tiles // group)),
            ],
            input_output_aliases={6: 0, 7: 1} if outs else {},
            cost_estimate=cost,
            compiler_params=params,
            name=f"spread{s}",
        )(scalars, before, rank, prefix, tables[s], tails[s], *outs)
    return tuple(outs)


def solution(mesh):
    return jax.shard_map(
        functools.partial(per_device, mesh.shape["rows"]),
        mesh=mesh,
        in_specs=(P(None, None, "rows"), P(None, "rows")),
        out_specs=(P(None, None, "rows"), P(None, None, "rows")),
        check_vma=False,
    )
```

time: 103 us -> 51.5 us (0.50)
  the two profiles are of different devices: /device:TPU:0 before, /device:TPU:8 now
where the time goes in v2:
time: 51.5 us; the launch traced here: 51.2 us
  Pallas kernels  30 us (58%)
  starting transfers between devices  10.1 us (20%)
  waiting for transfers between devices  6.62 us (13%)
  local copies, waits for them, and re-layouts  3.68 us (7%)
  between operations  0.78 us (2%)
    pallas_call x1, Pallas kernels, per_device(): pl.pallas_call(functools.partial(head_kernel, count, tiles, group), in_sp...  12.6 us
    pallas_call x4, Pallas kernels, per_device(): pl.pallas_call(functools.partial(spread_kernel, s, tiles, group), in_spec...  10.8 us
    ppermute x4, starting transfers between devices, per_device(): lax.ppermute(send, 'rows', [(i, i + 1) for i in range(count - 1)])  10.1 us
    ppermute x4, waiting for transfers between devices, per_device(): lax.ppermute(send, 'rows', [(i, i + 1) for i in range(count - 1)])  6.62 us
    pallas_call x4, Pallas kernels, per_device(): pl.pallas_call(functools.partial(pack_kernel, s, tiles), in_specs=[smem,...  5.67 us
    unnamed x10, local copies, waits for them, and re-layouts  3.68 us
  transfers between devices with their start and end apart: 4, of which 3 were waited for; matrix products, arithmetic and copies ran while one was open for 0% of the time, Pallas kernels for 24%

profile of v2, /device:TPU:8, one launch (start us, length us, event | category | flops | bytes accessed | tf_op | source)
XLA Modules:
  0.0 51.2 jit_solution(16239464119114295619)
XLA Ops:
  0.6 0.0 copy-start.3
  0.6 0.9 %copy-done.3 = s32[4,8192]{1,0:T(4,128)S(1)} copy-done((s32[4,8192]{1,0:T(4,128)S(1)}, s32[4,8192]{1,0:T(4,128)}, u32[]{:S(2)}) %copy-start.3) | copy-done | bytes 131096
  1.5 1.0 %index.1 = (s32[256,128]{1,0:T(8,128)S(1)}, s32[256,128]{1,0:T(8,128)S(1)}, s32[8,256]{1,0:T(8,128)S(1)}) custom-call(s32[4,8192]{1,0:T(4,128)S(1)} %copy-done.3), custom_call_target="tpu_custom_call" | custom-call | tf_op jit(solution)/shard_map/index/pallas_call | solution.py:263
  2.5 0.0 copy-start.1
  2.5 0.6 %copy-done.1 = s32[8,256]{1,0:T(8,128)} copy-done((s32[8,256]{1,0:T(8,128)}, s32[8,256]{1,0:T(8,128)S(1)}, u32[]{:S(2)}) %copy-start.1) | copy-done | bytes 8216
  3.1 0.0 copy-start.2
  3.1 12.6 %head.1 = (f32[256,32,128]{2,1,0:T(8,128)}, f32[8,128]{1,0:T(8,128)}) custom-call(s32[8,256]{1,0:T(8,128)} %copy-done.1, f32[4,32,8192]{2,1,0:T(8,128)} %events_ref.1, s32[4,8192]{1,0:T(4,128)} %keep_ref.3), custom_call_target="tpu_custom_call" | custom-call | tf_op jit(solution)/shard_map/head/pallas_call | solution.py:275
  15.8 0.0 copy-done.2
  15.8 0.0 copy-start
  15.8 2.2 %copy-done = f32[256,32,128]{2,1,0:T(8,128)S(1)} copy-done((f32[256,32,128]{2,1,0:T(8,128)S(1)}, f32[256,32,128]{2,1,0:T(8,128)}, u32[]{:S(2)}) %copy-start) | copy-done | bytes 4194328
  18.0 1.4 %pack0.1 = (f32[66,32,128]{2,1,0:T(8,128)S(1)}, f32[32,32,128]{2,1,0:T(8,128)S(1)}) custom-call(s32[8,256]{1,0:T(8,128)S(1)} %copy-done.2, f32[256,32,128]{2,1,0:T(8,128)S(1)} %copy-done, s32[256,128]{1,0:T(8,128)S(1)} %get-tuple-element.25.slot_ref), custom_call_target="tpu_custom_call" | custom-call | flops 100000000 | bytes 8388608 | tf_op jit(solution)/shard_map/pack0/pallas_call | solution.py:297
  19.4 2.0 %collective-permute-start.3 = (f32[32,32,128]{2,1,0:T(8,128)S(1)}, f32[32,32,128]{2,1,0:T(8,128)S(1)}, u32[]{:S(2)}, u32[]{:S(2)}) collective-permute-start(f32[32,32,128]{2,1,0:T(8,128)S(1)} %get-tuple-element.33), channel_id=1, source_target_pairs={{0,1},{1,2},{2,3},{3,4},{4,5},{5,6},{6,7},{7,8},{8,9},{9,10},{10,1... | collective-permute-start | bytes 1572872 | tf_op jit(solution)/shard_map/ppermute | solution.py:309
  21.4 1.4 %pack1.1 = (f32[66,32,128]{2,1,0:T(8,128)S(1)}, f32[32,32,128]{2,1,0:T(8,128)S(1)}) custom-call(s32[8,256]{1,0:T(8,128)S(1)} %copy-done.2, f32[256,32,128]{2,1,0:T(8,128)S(1)} %copy-done, s32[256,128]{1,0:T(8,128)S(1)} %get-tuple-element.25.slot_ref, f32[66,32,128]{2,1,0:T(8,128)S(1)} %get-tuple-element.26.rest_0_.table_ref), custom_call_target="tpu_custom_call" | custom-call | flops 100000000 | bytes 8388608 | tf_op jit(solution)/shard_map/pack1/pallas_call | solution.py:297
  22.8 2.5 %collective-permute-start.2 = (f32[32,32,128]{2,1,0:T(8,128)S(1)}, f32[32,32,128]{2,1,0:T(8,128)S(1)}, u32[]{:S(2)}, u32[]{:S(2)}) collective-permute-start(f32[32,32,128]{2,1,0:T(8,128)S(1)} %get-tuple-element.32), channel_id=1, source_target_pairs={{0,1},{1,2},{2,3},{3,4},{4,5},{5,6},{6,7},{7,8},{8,9},{9,10},{10,1... | collective-permute-start | bytes 1572872 | tf_op jit(solution)/shard_map/ppermute | solution.py:309
  25.3 0.0 copy-start.4
  25.4 1.4 %pack2.1 = (f32[66,32,128]{2,1,0:T(8,128)S(1)}, f32[32,32,128]{2,1,0:T(8,128)S(1)}) custom-call(s32[8,256]{1,0:T(8,128)S(1)} %copy-done.2, f32[256,32,128]{2,1,0:T(8,128)S(1)} %copy-done, s32[256,128]{1,0:T(8,128)S(1)} %get-tuple-element.25.slot_ref, f32[66,32,128]{2,1,0:T(8,128)S(1)} %get-tuple-element.27.rest_0_.table_ref), custom_call_target="tpu_custom_call" | custom-call | flops 100000000 | bytes 8388608 | tf_op jit(solution)/shard_map/pack2/pallas_call | solution.py:297
  26.8 2.1 %collective-permute-start.1 = (f32[32,32,128]{2,1,0:T(8,128)S(1)}, f32[32,32,128]{2,1,0:T(8,128)S(1)}, u32[]{:S(2)}, u32[]{:S(2)}) collective-permute-start(f32[32,32,128]{2,1,0:T(8,128)S(1)} %get-tuple-element.31), channel_id=1, source_target_pairs={{0,1},{1,2},{2,3},{3,4},{4,5},{5,6},{6,7},{7,8},{8,9},{9,10},{10,1... | collective-permute-start | bytes 1572872 | tf_op jit(solution)/shard_map/ppermute | solution.py:309
  28.9 1.4 %pack3.1 = (f32[66,32,128]{2,1,0:T(8,128)S(1)}, f32[32,32,128]{2,1,0:T(8,128)S(1)}) custom-call(s32[8,256]{1,0:T(8,128)S(1)} %copy-done.2, f32[256,32,128]{2,1,0:T(8,128)S(1)} %copy-done, s32[256,128]{1,0:T(8,128)S(1)} %get-tuple-element.25.slot_ref, f32[66,32,128]{2,1,0:T(8,128)S(1)} %get-tuple-element.28.rest_0_.table_ref), custom_call_target="tpu_custom_call" | custom-call | flops 100000000 | bytes 8388608 | tf_op jit(solution)/shard_map/pack3/pallas_call | solution.py:297
  30.3 3.5 %collective-permute-start = (f32[32,32,128]{2,1,0:T(8,128)S(1)}, f32[32,32,128]{2,1,0:T(8,128)S(1)}, u32[]{:S(2)}, u32[]{:S(2)}) collective-permute-start(f32[32,32,128]{2,1,0:T(8,128)S(1)} %get-tuple-element.30), channel_id=1, source_target_pairs={{0,1},{1,2},{2,3},{3,4},{4,5},{5,6},{6,7},{7,8},{8,9},{9,10},{10,1... | collective-permute-start | bytes 1572872 | tf_op jit(solution)/shard_map/ppermute | solution.py:309
  33.8 0.0 collective-permute-done.3.tail_ref
  33.8 0.0 copy-done.4
  33.8 2.7 %spread0.1 = (f32[4,32,8192]{2,1,0:T(8,128)}, f32[4,32,8192]{2,1,0:T(8,128)}) custom-call(s32[8,256]{1,0:T(8,128)S(1)} %copy-done.2, f32[8,128]{1,0:T(8,128)S(1)} %copy-done.4, s32[256,128]{1,0:T(8,128)S(1)} %get-tuple-element.23.rank_ref, f32[256,32,128]{2,1,0:T(8,128)S(1)} %copy-done, f32[66,32,128]{2,1,0:T(8,128)S(1)} %get-tuple-element.26.rest_0_.table_ref, ...), custom_call_target="tpu_custom_call" | custom-call | flops 100000000 | bytes 8388608 | tf_op jit(solution)/shard_map/spread0/pallas_call | solution.py:314
  36.5 0.8 %collective-permute-done.2.tail_ref = f32[32,32,128]{2,1,0:T(8,128)S(1)} collective-permute-done((f32[32,32,128]{2,1,0:T(8,128)S(1)}, f32[32,32,128]{2,1,0:T(8,128)S(1)}, u32[]{:S(2)}, u32[]{:S(2)}) %collective-permute-start.2) | collective-permute-done | bytes 524320 | tf_op jit(solution)/shard_map/ppermute | solution.py:309
  37.3 2.7 %spread1.1 = (f32[4,32,8192]{2,1,0:T(8,128)}, f32[4,32,8192]{2,1,0:T(8,128)}) custom-call(s32[8,256]{1,0:T(8,128)S(1)} %copy-done.2, f32[8,128]{1,0:T(8,128)S(1)} %copy-done.4, s32[256,128]{1,0:T(8,128)S(1)} %get-tuple-element.23.rank_ref, f32[256,32,128]{2,1,0:T(8,128)S(1)} %copy-done, ...), custom_call_target="tpu_custom_call", output_to_operand_aliasing={{0}: (6, {}), {1}: (7, {})} | custom-call | flops 100000000 | bytes 8388608 | tf_op jit(solution)/shard_map/spread1/pallas_call | solution.py:314
  40.0 2.9 %collective-permute-done.1.tail_ref = f32[32,32,128]{2,1,0:T(8,128)S(1)} collective-permute-done((f32[32,32,128]{2,1,0:T(8,128)S(1)}, f32[32,32,128]{2,1,0:T(8,128)S(1)}, u32[]{:S(2)}, u32[]{:S(2)}) %collective-permute-start.1) | collective-permute-done | bytes 524320 | tf_op jit(solution)/shard_map/ppermute | solution.py:309
  42.9 2.7 %spread2.1 = (f32[4,32,8192]{2,1,0:T(8,128)}, f32[4,32,8192]{2,1,0:T(8,128)}) custom-call(s32[8,256]{1,0:T(8,128)S(1)} %copy-done.2, f32[8,128]{1,0:T(8,128)S(1)} %copy-done.4, s32[256,128]{1,0:T(8,128)S(1)} %get-tuple-element.23.rank_ref, f32[256,32,128]{2,1,0:T(8,128)S(1)} %copy-done, ...), custom_call_target="tpu_custom_call", output_to_operand_aliasing={{0}: (6, {}), {1}: (7, {})} | custom-call | flops 100000000 | bytes 8388608 | tf_op jit(solution)/shard_map/spread2/pallas_call | solution.py:314
  45.6 2.9 %collective-permute-done.tail_ref = f32[32,32,128]{2,1,0:T(8,128)S(1)} collective-permute-done((f32[32,32,128]{2,1,0:T(8,128)S(1)}, f32[32,32,128]{2,1,0:T(8,128)S(1)}, u32[]{:S(2)}, u32[]{:S(2)}) %collective-permute-start) | collective-permute-done | bytes 524320 | tf_op jit(solution)/shard_map/ppermute | solution.py:309
  48.5 2.7 %spread3.1 = (f32[4,32,8192]{2,1,0:T(8,128)}, f32[4,32,8192]{2,1,0:T(8,128)}) custom-call(s32[8,256]{1,0:T(8,128)S(1)} %copy-done.2, f32[8,128]{1,0:T(8,128)S(1)} %copy-done.4, s32[256,128]{1,0:T(8,128)S(1)} %get-tuple-element.23.rank_ref, f32[256,32,128]{2,1,0:T(8,128)S(1)} %copy-done, ...), custom_call_target="tpu_custom_call", output_to_operand_aliasing={{0}: (6, {}), {1}: (7, {})} | custom-call | flops 100000000 | bytes 8388608 | tf_op jit(solution)/shard_map/spread3/pallas_call | solution.py:314
Async XLA Ops:
  0.6 0.9 %copy-start.3 = (s32[4,8192]{1,0:T(4,128)S(1)}, s32[4,8192]{1,0:T(4,128)}, u32[]{:S(2)}) copy-start(s32[4,8192]{1,0:T(4,128)} %keep_ref.3) | copy-start | bytes 393220
  2.5 0.6 %copy-start.1 = (s32[8,256]{1,0:T(8,128)}, s32[8,256]{1,0:T(8,128)S(1)}, u32[]{:S(2)}) copy-start(s32[8,256]{1,0:T(8,128)S(1)} %get-tuple-element.21.scalars_ref) | copy-start | bytes 24580
  3.1 12.6 %copy-start.2 = (s32[8,256]{1,0:T(8,128)S(1)}, s32[8,256]{1,0:T(8,128)}, u32[]{:S(2)}) copy-start(s32[8,256]{1,0:T(8,128)} %copy-done.1) | copy-start | bytes 24580
  15.8 2.2 %copy-start = (f32[256,32,128]{2,1,0:T(8,128)S(1)}, f32[256,32,128]{2,1,0:T(8,128)}, u32[]{:S(2)}) copy-start(f32[256,32,128]{2,1,0:T(8,128)} %get-tuple-element.24.prefix_ref) | copy-start | bytes 12582916
  19.4 14.4 %collective-permute-start.3 = (f32[32,32,128]{2,1,0:T(8,128)S(1)}, f32[32,32,128]{2,1,0:T(8,128)S(1)}, u32[]{:S(2)}, u32[]{:S(2)}) collective-permute-start(f32[32,32,128]{2,1,0:T(8,128)S(1)} %get-tuple-element.33), channel_id=1, source_target_pairs={{0,1},{1,2},{2,3},{3,4},{4,5},{5,6},{6,7},{7,8},{8,9},{9,10},{10,1... | collective-permute-start | bytes 1572872 | tf_op jit(solution)/shard_map/ppermute | solution.py:309
  22.8 14.5 %collective-permute-start.2 = (f32[32,32,128]{2,1,0:T(8,128)S(1)}, f32[32,32,128]{2,1,0:T(8,128)S(1)}, u32[]{:S(2)}, u32[]{:S(2)}) collective-permute-start(f32[32,32,128]{2,1,0:T(8,128)S(1)} %get-tuple-element.32), channel_id=1, source_target_pairs={{0,1},{1,2},{2,3},{3,4},{4,5},{5,6},{6,7},{7,8},{8,9},{9,10},{10,1... | collective-permute-start | bytes 1572872 | tf_op jit(solution)/shard_map/ppermute | solution.py:309
  25.3 8.5 %copy-start.4 = (f32[8,128]{1,0:T(8,128)S(1)}, f32[8,128]{1,0:T(8,128)}, u32[]{:S(2)}) copy-start(f32[8,128]{1,0:T(8,128)} %get-tuple-element.22.before_ref) | copy-start | bytes 12292
  26.8 16.1 %collective-permute-start.1 = (f32[32,32,128]{2,1,0:T(8,128)S(1)}, f32[32,32,128]{2,1,0:T(8,128)S(1)}, u32[]{:S(2)}, u32[]{:S(2)}) collective-permute-start(f32[32,32,128]{2,1,0:T(8,128)S(1)} %get-tuple-element.31), channel_id=1, source_target_pairs={{0,1},{1,2},{2,3},{3,4},{4,5},{5,6},{6,7},{7,8},{8,9},{9,10},{10,1... | collective-permute-start | bytes 1572872 | tf_op jit(solution)/shard_map/ppermute | solution.py:309
  30.3 18.2 %collective-permute-start = (f32[32,32,128]{2,1,0:T(8,128)S(1)}, f32[32,32,128]{2,1,0:T(8,128)S(1)}, u32[]{:S(2)}, u32[]{:S(2)}) collective-permute-start(f32[32,32,128]{2,1,0:T(8,128)S(1)} %get-tuple-element.30), channel_id=1, source_target_pairs={{0,1},{1,2},{2,3},{3,4},{4,5},{5,6},{6,7},{7,8},{8,9},{9,10},{10,1... | collective-permute-start | bytes 1572872 | tf_op jit(solution)/shard_map/ppermute | solution.py:309

commit v3 on v2

v3 whole, which is shorter than its diff:
```python
import functools

import jax
import jax.numpy as jnp
from jax import lax
from jax.experimental import pallas as pl
from jax.experimental.pallas import tpu as pltpu
from jax.sharding import PartitionSpec as P

SPAN = 4096
LANES = 128
GROUP = 16
GRANT = 8 * 2**20
GATHERED = 2**20
F32, BF16, I32 = jnp.float32, jnp.bfloat16, jnp.int32


def iota(shape, axis):
    return lax.broadcasted_iota(I32, shape, axis)


def lane_gather(values, index):
    return jnp.take_along_axis(values, index, axis=1, mode="promise_in_bounds")


def prepare_kernel(tiles, events_hbm, keep_hbm, events_ref, keep_ref, rank_ref, slot_ref, scalars_ref, mine_ref, flags, sems):
    streams, cols, _ = events_ref.shape
    rows = streams * tiles
    flag_load = pltpu.make_async_copy(keep_hbm, keep_ref, sems.at[streams])
    flag_load.start()
    loads = [pltpu.make_async_copy(events_hbm.at[s], events_ref.at[s], sems.at[s]) for s in range(streams)]
    for load in loads:
        load.start()
    flag_load.wait()
    for s in range(streams):
        for t in range(tiles):
            flags[s * tiles + t : s * tiles + t + 1, :] = keep_ref[s : s + 1, t * LANES : (t + 1) * LANES]
    kept = flags[...].astype(F32).astype(BF16)
    square = (LANES, LANES)
    upper = (iota(square, 0) <= iota(square, 1)).astype(F32).astype(BF16)
    ones = jnp.ones(square, BF16)
    within = jnp.dot(kept, upper, preferred_element_type=F32)
    counts = jnp.dot(kept, ones, preferred_element_type=F32).astype(BF16)
    grid = (rows, rows)
    same = (iota(grid, 0) // tiles) == (iota(grid, 1) // tiles)
    below = (same & (iota(grid, 1) < iota(grid, 0))).astype(F32).astype(BF16)
    above = (same & (iota(grid, 0) < iota(grid, 1))).astype(F32).astype(BF16)
    start = jnp.dot(below, counts, preferred_element_type=F32).astype(I32)
    within = within.astype(I32)
    rank_ref[...] = start + within
    lane = iota((rows, LANES), 1)
    wanted = ((lane - start - 1) & (LANES - 1)) + 1
    position = jnp.zeros((rows, LANES), I32)
    step = LANES // 2
    while step:
        seen = lane_gather(within, position + (step - 1))
        position = jnp.where(seen < wanted, position + step, position)
        step //= 2
    slot_ref[...] = position
    contract = (((1,), (1,)), ((), ()))
    first = (iota((8, LANES), 1) == 0).astype(F32).astype(BF16)
    count_row = lax.dot_general(jnp.ones((8, LANES), BF16), kept, contract, preferred_element_type=F32)
    first_row = lax.dot_general(first, kept, contract, preferred_element_type=F32)
    count_row = count_row.astype(BF16)
    start_row = jnp.dot(count_row, above, preferred_element_type=F32)
    total_row = jnp.dot(count_row, same.astype(F32).astype(BF16), preferred_element_type=F32)
    which = iota((8, rows), 0)
    row = jnp.where(which == 0, start_row, jnp.where(which == 1, total_row, start_row + first_row))
    scalars_ref[...] = row.astype(I32)
    group = 8
    span = group * LANES
    totals = []
    for s in range(streams):
        loads[s].wait()

        def add(g, total, s=s):
            columns = pl.ds(pl.multiple_of(g * span, span), span)
            values = jnp.where(keep_ref[s : s + 1, columns] != 0, events_ref[s, :, columns], 0.0)
            parts = [values[:, i * LANES : (i + 1) * LANES] for i in range(group)]
            while len(parts) > 1:
                parts = [parts[i] + parts[i + 1] for i in range(0, len(parts), 2)]
            return total + parts[0]

        totals.append(lax.fori_loop(0, tiles // group, add, jnp.zeros((cols, LANES), F32), unroll=True))
    sums = lax.dot_general(
        jnp.ones((8, LANES), F32),
        jnp.concatenate(totals, axis=0),
        contract,
        precision=lax.Precision.HIGHEST,
        preferred_element_type=F32,
    )
    width = streams * cols
    line, column = iota((8, width), 0), iota((8, width), 1)
    tallies = jnp.zeros((8, width), F32)
    for s in range(streams):
        tallies = jnp.where(column // cols == s, total_row[:, s * tiles : s * tiles + 1], tallies)
    mine_ref[...] = jnp.zeros(mine_ref.shape, F32)
    mine_ref[0:8, :] = jnp.where(line == 0, sums, tallies)


def pack_kernel(s, tiles, group, scalars_ref, events_ref, keep_ref, slot_ref, *rest):
    prefix_ref, table_ref, send_ref = rest[-3:]
    cols = prefix_ref.shape[1]
    lane = iota((cols, LANES), 1)
    shape = (2 * LANES, 2 * LANES)
    weights = (((iota(shape, 0) & (LANES - 1)) <= iota(shape, 1)).astype(F32)).astype(BF16)
    total = jnp.zeros((cols, LANES), F32)
    current = jnp.zeros((cols, LANES), F32)
    for g in range(tiles // group):
        left, right = [], []
        for i in range(group):
            columns = slice((g * group + i) * LANES, (g * group + i + 1) * LANES)
            values = jnp.where(keep_ref[s : s + 1, columns] != 0, events_ref[s, :, columns], 0.0)
            high = values.astype(BF16)
            left.append(high)
            right.append((values - high.astype(F32)).astype(BF16))
        pair = jnp.concatenate([jnp.concatenate(left, axis=0), jnp.concatenate(right, axis=0)], axis=1)
        sums = jnp.dot(pair, weights, preferred_element_type=F32)
        for i in range(group):
            t = g * group + i
            piece = sums[i * cols : (i + 1) * cols]
            running = piece[:, :LANES] + total
            total = total + piece[:, LANES:]
            prefix_ref[t] = running
            order = jnp.broadcast_to(slot_ref[s * tiles + t : s * tiles + t + 1, :], (cols, LANES))
            packed = lane_gather(running, order)
            begin = scalars_ref[0, s * tiles + t] + 1
            block = begin // LANES
            merged = jnp.where(lane >= begin - block * LANES, packed, current)
            table_ref[block] = merged
            if t == tiles - 1:
                table_ref[block + 1] = packed
            else:
                following = (scalars_ref[0, s * tiles + t + 1] + 1) // LANES
                current = jnp.where(following > block, packed, merged)
    base = scalars_ref[1, s * tiles] - SPAN
    origin = base // LANES
    offset = base - origin * LANES
    turn = (lane + offset) & (LANES - 1)
    below = table_ref[origin]
    for m in range(SPAN // LANES):
        above = table_ref[origin + m + 1]
        send_ref[m] = lane_gather(jnp.where(lane >= offset, below, above), turn) - total
        below = above


def spread_kernel(s, tiles, group, scalars_ref, before_ref, rank_ref, prefix_ref, table_ref, tail_ref, *rest):
    mean_ref, deviation_ref, means, deviations, inverse, sems = rest[-6:]
    cols = prefix_ref.shape[1]
    back = SPAN // LANES
    width = before_ref.shape[1]
    mine = iota((cols, width), 1) == iota((cols, width), 0) + s * cols
    column = jnp.sum(jnp.where(mine, before_ref[0:1, :], 0.0), axis=1, keepdims=True)
    before = jnp.broadcast_to(column, (cols, LANES))
    first = iota((1, width), 1) == s * cols
    earlier = jnp.sum(jnp.where(first, before_ref[1:2, :], 0.0), axis=1, keepdims=True)
    ranks = rank_ref[s * tiles : (s + 1) * tiles, :]
    inverse[...] = 1.0 / jnp.maximum(earlier + ranks.astype(F32), 1.0)
    lane = iota((cols, LANES), 1)

    def fetch(block):
        old = tail_ref[jnp.minimum(block, back - 1)]
        new = table_ref[jnp.maximum(block - back, 0)]
        return jnp.where(block < back, old, new)

    copies = []
    for g in range(tiles // group):
        for i in range(group):
            t = g * group + i
            begin = scalars_ref[2, s * tiles + t]
            block = begin // LANES
            mixed = jnp.where(lane >= begin - block * LANES, fetch(block), fetch(block + 1))
            order = jnp.broadcast_to(rank_ref[s * tiles + t : s * tiles + t + 1, :] & (LANES - 1), (cols, LANES))
            running = prefix_ref[t]
            mean = (running - lane_gather(mixed, order)) * (1.0 / SPAN)
            columns = slice(t * LANES, (t + 1) * LANES)
            means[:, columns] = mean
            deviations[:, columns] = mean - (running + before) * inverse[t : t + 1, :]
        part = pl.ds(g * group * LANES, group * LANES)
        for k, (source, target) in enumerate(((means, mean_ref), (deviations, deviation_ref))):
            copy = pltpu.make_async_copy(source.at[:, part], target.at[s, :, part], sems.at[k, g])
            copy.start()
            copies.append(copy)
    for copy in copies:
        copy.wait()


def per_device(count, events, keep):
    streams, cols, rows = events.shape
    tiles = rows // LANES
    back = SPAN // LANES
    everything = streams * tiles
    width = streams * cols
    group = min(GROUP, tiles)
    smem = pl.BlockSpec(memory_space=pltpu.SMEM)
    vmem = pl.BlockSpec(memory_space=pltpu.VMEM)
    hbm = pl.BlockSpec(memory_space=pltpu.HBM)
    anywhere = pl.BlockSpec(memory_space=pl.ANY)
    cost = pl.CostEstimate(flops=10**8, bytes_accessed=8 * 2**20, transcendentals=0)
    params = pltpu.CompilerParams(vmem_limit_bytes=GRANT)
    lines = 8 * pl.cdiv(GATHERED, count * width * 4 * 8)

    events, keep, rank, slot, scalars, mine = pl.pallas_call(
        functools.partial(prepare_kernel, tiles),
        in_specs=[hbm, hbm],
        out_specs=[vmem] * 6,
        out_shape=(
            jax.ShapeDtypeStruct(events.shape, F32),
            jax.ShapeDtypeStruct(keep.shape, I32),
            jax.ShapeDtypeStruct((everything, LANES), I32),
            jax.ShapeDtypeStruct((everything, LANES), I32),
            jax.ShapeDtypeStruct((8, everything), I32),
            jax.ShapeDtypeStruct((lines, width), F32),
        ),
        scratch_shapes=[pltpu.VMEM((everything, LANES), I32), pltpu.SemaphoreType.DMA((streams + 1,))],
        compiler_params=params,
        name="prepare",
    )(events, keep)
    gathered = lax.all_gather(mine, "rows", axis=0, tiled=True).reshape(count, lines, width)[:, :8]
    earlier = jnp.arange(count, dtype=I32) < lax.axis_index("rows")
    before = jnp.sum(jnp.where(earlier[:, None, None], gathered, 0.0), axis=0)

    prefixes, tables, tails = [], [], []
    for s in range(streams):
        prefix, table, send = pl.pallas_call(
            functools.partial(pack_kernel, s, tiles, group),
            in_specs=[smem, vmem, vmem, vmem] + [anywhere] * (s > 0),
            out_specs=[vmem, vmem, vmem],
            out_shape=[
                jax.ShapeDtypeStruct((tiles, cols, LANES), F32),
                jax.ShapeDtypeStruct((tiles + 2, cols, LANES), F32),
                jax.ShapeDtypeStruct((back, cols, LANES), F32),
            ],
            cost_estimate=cost,
            compiler_params=params,
            name=f"pack{s}",
        )(scalars, events, keep, slot, *tables[-1:])
        tails.append(lax.ppermute(send, "rows", [(i, i + 1) for i in range(count - 1)]))
        prefixes.append(prefix)
        tables.append(table)

    outs = ()
    shape = (streams, cols, rows)
    for s in range(streams):
        outs = pl.pallas_call(
            functools.partial(spread_kernel, s, tiles, group),
            in_specs=[smem] + [vmem] * 5 + [anywhere] * len(outs),
            out_specs=[anywhere] * 2,
            out_shape=[jax.ShapeDtypeStruct(shape, F32)] * 2,
            scratch_shapes=[
                pltpu.VMEM((cols, rows), F32),
                pltpu.VMEM((cols, rows), F32),
                pltpu.VMEM((tiles, LANES), F32),
                pltpu.SemaphoreType.DMA((2, tiles // group)),
            ],
            input_output_aliases={6: 0, 7: 1} if outs else {},
            cost_estimate=cost,
            compiler_params=params,
            name=f"spread{s}",
        )(scalars, before, rank, prefixes[s], tables[s], tails[s], *outs)
    return tuple(outs)


def solution(mesh):
    return jax.shard_map(
        functools.partial(per_device, mesh.shape["rows"]),
        mesh=mesh,
        in_specs=(P(None, None, "rows"), P(None, "rows")),
        out_specs=(P(None, None, "rows"), P(None, None, "rows")),
        check_vma=False,
    )
```

time: 51.5 us -> 97.9 us (1.90)
  the two profiles are of different devices: /device:TPU:8 before, /device:TPU:0 now
where the time goes in v3:
time: 97.9 us; the launch traced here: 97.4 us
  waiting for transfers between devices  27.9 us (28%)
  Pallas kernels  25.4 us (26%)
  local copies, waits for them, and re-layouts  15.6 us (16%)
  between operations  14.2 us (15%)
  starting transfers between devices  13.2 us (13%)
  other arithmetic  1.01 us (1%)
    all_gather x1, waiting for transfers between devices, per_device(): lax.all_gather(mine, 'rows', axis=0, tiled=True)  27.9 us
    unnamed x32, local copies, waits for them, and re-layouts  15.6 us
    ppermute x4, starting transfers between devices, per_device(): lax.ppermute(send, 'rows', [(i, i + 1) for i in range(count - 1)])  13.2 us
    pallas_call x4, Pallas kernels, per_device(): pl.pallas_call(functools.partial(spread_kernel, s, tiles, group), in_spec...  12.5 us
    pallas_call x4, Pallas kernels, per_device(): pl.pallas_call(functools.partial(pack_kernel, s, tiles, group), in_specs=...  10.2 us
    pallas_call x1, Pallas kernels, per_device(): pl.pallas_call(functools.partial(prepare_kernel, tiles), in_specs=[hbm, h...  2.71 us
  transfers between devices with their start and end apart: 5, of which 1 were waited for; matrix products, arithmetic and copies ran while one was open for 1% of the time, Pallas kernels for 20%

profile of v3, /device:TPU:0, one launch (start us, length us, event | category | flops | bytes accessed | tf_op | source)
XLA Modules:
  0.0 97.4 jit_solution(11735059511546522388)
XLA Ops:
  7.2 0.0 all-gather.2.cloned.1.call-start
  7.2 2.2 %copy-done.2 = f32[4,32,8192]{2,1,0:T(8,128)S(1)} copy-done((f32[4,32,8192]{2,1,0:T(8,128)S(1)}, f32[4,32,8192]{2,1,0:T(8,128)}, u32[]{:S(2)}) %copy-start.2) | copy-done | bytes 4194328
  9.4 0.9 copy-done.15
  10.3 2.7 %prepare.1 = (f32[4,32,8192]{2,1,0:T(8,128)S(1)}, s32[4,8192]{1,0:T(4,128)S(1)}, s32[256,128]{1,0:T(8,128)S(1)}, s32[256,128]{1,0:T(8,128)S(1)}, s32[8,256]{1,0:T(8,128)S(1)}, /*index=5*/f32[64,128]{1,0:T(8,128)}) custom-call(f32[4,32,8192]{2,1,0:T(8,128)S(1)} %copy-done.2, s32[4,8192]{1,0:T(4,128)S(1)} %copy-done.15), custom_call_target="tpu_custom_call" | custom-call | tf_op jit(solution)/shard_map/prepare/pallas_call | solution.py:203
  13.0 0.0 copy-start
  13.0 2.0 %copy-done = f32[4,32,8192]{2,1,0:T(8,128)} copy-done((f32[4,32,8192]{2,1,0:T(8,128)}, f32[4,32,8192]{2,1,0:T(8,128)S(1)}, u32[]{:S(2)}) %copy-start) | copy-done | bytes 4194328
  15.0 0.0 all-gather.2.cloned.1.call-update
  15.1 0.0 copy-start.1
  15.1 2.2 %copy-done.1 = f32[4,32,8192]{2,1,0:T(8,128)S(1)} copy-done((f32[4,32,8192]{2,1,0:T(8,128)S(1)}, f32[4,32,8192]{2,1,0:T(8,128)}, u32[]{:S(2)}) %copy-start.1) | copy-done | bytes 4194328
  17.3 2.6 %pack0.1 = (f32[64,32,128]{2,1,0:T(8,128)S(1)}, f32[66,32,128]{2,1,0:T(8,128)S(1)}, f32[32,32,128]{2,1,0:T(8,128)}) custom-call(s32[8,256]{1,0:T(8,128)S(1)} %get-tuple-element.26.scalars_ref, f32[4,32,8192]{2,1,0:T(8,128)S(1)} %copy-done.1, s32[4,8192]{1,0:T(4,128)S(1)} %get-tuple-element.30.keep_ref, s32[256,128]{1,0:T(8,128)S(1)} %get-tuple-element.31.slot_ref), custom_call_target="tpu_custom_call" | custom-call | flops 100000000 | bytes 8388608 | tf_op jit(solution)/shard_map/pack0/pallas_call | solution.py:225
  19.9 1.0 copy-done.13
  20.8 3.2 %collective-permute-start.3 = (f32[32,32,128]{2,1,0:T(8,128)}, f32[32,32,128]{2,1,0:T(8,128)}, u32[]{:S(2)}, u32[]{:S(2)}) collective-permute-start(f32[32,32,128]{2,1,0:T(8,128)} %get-tuple-element.43), channel_id=1, source_target_pairs={{0,1},{1,2},{2,3},{3,4},{4,5},{5,6},{6,7},{7,8},{8,9},{9,10},{10,1... | collective-permute-start | bytes 1572872 | tf_op jit(solution)/shard_map/ppermute | solution.py:238
  24.0 2.5 %pack1.1 = (f32[64,32,128]{2,1,0:T(8,128)S(1)}, f32[66,32,128]{2,1,0:T(8,128)S(1)}, f32[32,32,128]{2,1,0:T(8,128)}) custom-call(s32[8,256]{1,0:T(8,128)S(1)} %get-tuple-element.26.scalars_ref, f32[4,32,8192]{2,1,0:T(8,128)S(1)} %copy-done.1, s32[4,8192]{1,0:T(4,128)S(1)} %get-tuple-element.30.keep_ref, s32[256,128]{1,0:T(8,128)S(1)} %get-tuple-element.31.slot_ref, ...), custom_call_target="tpu_custom_call" | custom-call | flops 100000000 | bytes 8388608 | tf_op jit(solution)/shard_map/pack1/pallas_call | solution.py:225
  26.6 1.0 %copy-done.11 = f32[64,32,128]{2,1,0:T(8,128)} copy-done((f32[64,32,128]{2,1,0:T(8,128)}, f32[64,32,128]{2,1,0:T(8,128)S(1)}, u32[]{:S(2)}) %copy-start.11) | copy-done | bytes 1048600
  27.6 4.5 %collective-permute-start.2 = (f32[32,32,128]{2,1,0:T(8,128)}, f32[32,32,128]{2,1,0:T(8,128)}, u32[]{:S(2)}, u32[]{:S(2)}) collective-permute-start(f32[32,32,128]{2,1,0:T(8,128)} %get-tuple-element.41), channel_id=1, source_target_pairs={{0,1},{1,2},{2,3},{3,4},{4,5},{5,6},{6,7},{7,8},{8,9},{9,10},{10,1... | collective-permute-start | bytes 1572872 | tf_op jit(solution)/shard_map/ppermute | solution.py:238
  32.0 0.9 copy-done.4
  33.0 2.5 %pack2.1 = (f32[64,32,128]{2,1,0:T(8,128)S(1)}, f32[66,32,128]{2,1,0:T(8,128)S(1)}, f32[32,32,128]{2,1,0:T(8,128)}) custom-call(s32[8,256]{1,0:T(8,128)S(1)} %get-tuple-element.26.scalars_ref, f32[4,32,8192]{2,1,0:T(8,128)S(1)} %copy-done.1, s32[4,8192]{1,0:T(4,128)S(1)} %get-tuple-element.30.keep_ref, s32[256,128]{1,0:T(8,128)S(1)} %copy-done.4, ...), custom_call_target="tpu_custom_call" | custom-call | flops 100000000 | bytes 8388608 | tf_op jit(solution)/shard_map/pack2/pallas_call | solution.py:225
  35.5 1.0 %copy-done.9 = f32[64,32,128]{2,1,0:T(8,128)} copy-done((f32[64,32,128]{2,1,0:T(8,128)}, f32[64,32,128]{2,1,0:T(8,128)S(1)}, u32[]{:S(2)}) %copy-start.9) | copy-done | bytes 1048600
  36.5 2.2 %collective-permute-start.1 = (f32[32,32,128]{2,1,0:T(8,128)}, f32[32,32,128]{2,1,0:T(8,128)}, u32[]{:S(2)}, u32[]{:S(2)}) collective-permute-start(f32[32,32,128]{2,1,0:T(8,128)} %get-tuple-element.39), channel_id=1, source_target_pairs={{0,1},{1,2},{2,3},{3,4},{4,5},{5,6},{6,7},{7,8},{8,9},{9,10},{10,1... | collective-permute-start | bytes 1572872 | tf_op jit(solution)/shard_map/ppermute | solution.py:238
  38.7 2.6 %pack3.1 = (f32[64,32,128]{2,1,0:T(8,128)S(1)}, f32[66,32,128]{2,1,0:T(8,128)S(1)}, f32[32,32,128]{2,1,0:T(8,128)}) custom-call(s32[8,256]{1,0:T(8,128)S(1)} %get-tuple-element.26.scalars_ref, f32[4,32,8192]{2,1,0:T(8,128)S(1)} %copy-done.1, s32[4,8192]{1,0:T(4,128)S(1)} %get-tuple-element.30.keep_ref, s32[256,128]{1,0:T(8,128)S(1)} %copy-done.4, ...), custom_call_target="tpu_custom_call" | custom-call | flops 100000000 | bytes 8388608 | tf_op jit(solution)/shard_map/pack3/pallas_call | solution.py:225
  41.2 1.0 %copy-done.5 = f32[66,32,128]{2,1,0:T(8,128)} copy-done((f32[66,32,128]{2,1,0:T(8,128)}, f32[66,32,128]{2,1,0:T(8,128)S(1)}, u32[]{:S(2)}) %copy-start.5) | copy-done | bytes 1081368
  42.3 1.0 copy-done.7
  43.2 3.3 %collective-permute-start = (f32[32,32,128]{2,1,0:T(8,128)}, f32[32,32,128]{2,1,0:T(8,128)}, u32[]{:S(2)}, u32[]{:S(2)}) collective-permute-start(f32[32,32,128]{2,1,0:T(8,128)} %get-tuple-element.37), channel_id=1, source_target_pairs={{0,1},{1,2},{2,3},{3,4},{4,5},{5,6},{6,7},{7,8},{8,9},{9,10},{10,1... | collective-permute-start | bytes 1572872 | tf_op jit(solution)/shard_map/ppermute | solution.py:238
  46.5 27.9 %all-gather.2.cloned.1.call-done = f32[2048,128]{1,0:T(8,128)} async-done(((f32[64,128]{1,0:T(8,128)}), f32[2048,128]{1,0:T(8,128)}) %all-gather.2.cloned.1.call-update) | async-done | bytes 1048592 | tf_op jit(solution)/shard_map/all_gather | solution.py:219
  74.4 1.0 %fusion.before_ref = f32[8,128]{1,0:T(8,128)S(1)} fusion(f32[32,64,128]{2,1,0:T(8,128)} %bitcast.1, pred[32]{0:T(512)(128)(4,1)S(1)} %iota_compare_fusion), kind=kLoop, calls=%fused_computation.1 | loop fusion | flops 64512 | bytes 135200 | tf_op jit(solution)/shard_map/reduce_sum | solution.py:221
  75.5 0.0 copy-start.14
  75.5 1.2 %copy-done.14 = f32[64,32,128]{2,1,0:T(8,128)S(1)} copy-done((f32[64,32,128]{2,1,0:T(8,128)S(1)}, f32[64,32,128]{2,1,0:T(8,128)}, u32[]{:S(2)}) %copy-start.14) | copy-done | bytes 1048600
  76.7 3.1 %spread0.1 = (f32[4,32,8192]{2,1,0:T(8,128)}, f32[4,32,8192]{2,1,0:T(8,128)}) custom-call(s32[8,256]{1,0:T(8,128)S(1)} %get-tuple-element.26.scalars_ref, f32[8,128]{1,0:T(8,128)S(1)} %fusion.before_ref, s32[256,128]{1,0:T(8,128)S(1)} %get-tuple-element.28.rank_ref, f32[64,32,128]{2,1,0:T(8,128)S(1)} %copy-done.14, ...), custom_call_target="tpu_custom_call" | custom-call | flops 100000000 | bytes 8388608 | tf_op jit(solution)/shard_map/spread0/pallas_call | solution.py:245
  79.8 1.2 %copy-done.12 = f32[64,32,128]{2,1,0:T(8,128)S(1)} copy-done((f32[64,32,128]{2,1,0:T(8,128)S(1)}, f32[64,32,128]{2,1,0:T(8,128)}, u32[]{:S(2)}) %copy-start.12) | copy-done | bytes 1048600
  81.0 3.1 %spread1.1 = (f32[4,32,8192]{2,1,0:T(8,128)}, f32[4,32,8192]{2,1,0:T(8,128)}) custom-call(s32[8,256]{1,0:T(8,128)S(1)} %get-tuple-element.26.scalars_ref, f32[8,128]{1,0:T(8,128)S(1)} %fusion.before_ref, s32[256,128]{1,0:T(8,128)S(1)} %get-tuple-element.28.rank_ref, f32[64,32,128]{2,1,0:T(8,128)S(1)} %copy-done.12, ...), custom_call_target="tpu_custom_call", output_to_operand_aliasing={{0}: (6, {}), {1}: (7, {})} | custom-call | flops 100000000 | bytes 8388608 | tf_op jit(solution)/shard_map/spread1/pallas_call | solution.py:245
  84.2 3.2 %spread2.1 = (f32[4,32,8192]{2,1,0:T(8,128)}, f32[4,32,8192]{2,1,0:T(8,128)}) custom-call(s32[8,256]{1,0:T(8,128)S(1)} %get-tuple-element.26.scalars_ref, f32[8,128]{1,0:T(8,128)S(1)} %fusion.before_ref, s32[256,128]{1,0:T(8,128)S(1)} %get-tuple-element.28.rank_ref, f32[64,32,128]{2,1,0:T(8,128)S(1)} %copy-done.10, ...), custom_call_target="tpu_custom_call", output_to_operand_aliasing={{0}: (6, {}), {1}: (7, {})} | custom-call | flops 100000000 | bytes 8388608 | tf_op jit(solution)/shard_map/spread2/pallas_call | solution.py:245
  87.5 3.1 %spread3.1 = (f32[4,32,8192]{2,1,0:T(8,128)}, f32[4,32,8192]{2,1,0:T(8,128)}) custom-call(s32[8,256]{1,0:T(8,128)S(1)} %get-tuple-element.26.scalars_ref, f32[8,128]{1,0:T(8,128)S(1)} %fusion.before_ref, s32[256,128]{1,0:T(8,128)S(1)} %get-tuple-element.28.rank_ref, f32[64,32,128]{2,1,0:T(8,128)S(1)} %copy-done.8, ...), custom_call_target="tpu_custom_call", output_to_operand_aliasing={{0}: (6, {}), {1}: (7, {})} | custom-call | flops 100000000 | bytes 8388608 | tf_op jit(solution)/shard_map/spread3/pallas_call | solution.py:245
  (22 shorter events, 0.0 us)
Async XLA Ops:
  7.2 67.3 %all-gather.2.cloned.1.call-start = ((), (), s32[]{:S(2)}) async-start(), calls=%async_computation | async-start | bytes 1081344 | tf_op jit(solution)/shard_map/all_gather | solution.py:219
  7.2 2.2 %copy-start.2 = (f32[4,32,8192]{2,1,0:T(8,128)S(1)}, f32[4,32,8192]{2,1,0:T(8,128)}, u32[]{:S(2)}) copy-start(f32[4,32,8192]{2,1,0:T(8,128)} %events_hbm.1) | copy-start | bytes 12582916
  9.4 0.9 copy-start.15
  13.0 2.0 %copy-start = (f32[4,32,8192]{2,1,0:T(8,128)}, f32[4,32,8192]{2,1,0:T(8,128)S(1)}, u32[]{:S(2)}) copy-start(f32[4,32,8192]{2,1,0:T(8,128)S(1)} %get-tuple-element.29.events_ref) | copy-start | bytes 12582916
  15.0 11.5 %copy-start.3 = (s32[256,128]{1,0:T(8,128)}, s32[256,128]{1,0:T(8,128)S(1)}, u32[]{:S(2)}) copy-start(s32[256,128]{1,0:T(8,128)S(1)} %get-tuple-element.31.slot_ref) | copy-start | bytes 393220
  15.1 2.2 %copy-start.1 = (f32[4,32,8192]{2,1,0:T(8,128)S(1)}, f32[4,32,8192]{2,1,0:T(8,128)}, u32[]{:S(2)}) copy-start(f32[4,32,8192]{2,1,0:T(8,128)} %copy-done) | copy-start | bytes 12582916
  19.9 1.0 copy-start.13
  20.8 54.6 %collective-permute-start.3 = (f32[32,32,128]{2,1,0:T(8,128)}, f32[32,32,128]{2,1,0:T(8,128)}, u32[]{:S(2)}, u32[]{:S(2)}) collective-permute-start(f32[32,32,128]{2,1,0:T(8,128)} %get-tuple-element.43), channel_id=1, source_target_pairs={{0,1},{1,2},{2,3},{3,4},{4,5},{5,6},{6,7},{7,8},{8,9},{9,10},{10,1... | collective-permute-start | bytes 1572872 | tf_op jit(solution)/shard_map/ppermute | solution.py:238
  26.6 1.0 %copy-start.11 = (f32[64,32,128]{2,1,0:T(8,128)}, f32[64,32,128]{2,1,0:T(8,128)S(1)}, u32[]{:S(2)}) copy-start(f32[64,32,128]{2,1,0:T(8,128)S(1)} %get-tuple-element.40.prefix_ref) | copy-start | bytes 3145732
  27.6 52.2 %collective-permute-start.2 = (f32[32,32,128]{2,1,0:T(8,128)}, f32[32,32,128]{2,1,0:T(8,128)}, u32[]{:S(2)}, u32[]{:S(2)}) collective-permute-start(f32[32,32,128]{2,1,0:T(8,128)} %get-tuple-element.41), channel_id=1, source_target_pairs={{0,1},{1,2},{2,3},{3,4},{4,5},{5,6},{6,7},{7,8},{8,9},{9,10},{10,1... | collective-permute-start | bytes 1572872 | tf_op jit(solution)/shard_map/ppermute | solution.py:238
  32.0 0.9 copy-start.4
  35.5 1.0 %copy-start.9 = (f32[64,32,128]{2,1,0:T(8,128)}, f32[64,32,128]{2,1,0:T(8,128)S(1)}, u32[]{:S(2)}) copy-start(f32[64,32,128]{2,1,0:T(8,128)S(1)} %get-tuple-element.38.prefix_ref) | copy-start | bytes 3145732
  36.5 47.7 %collective-permute-start.1 = (f32[32,32,128]{2,1,0:T(8,128)}, f32[32,32,128]{2,1,0:T(8,128)}, u32[]{:S(2)}, u32[]{:S(2)}) collective-permute-start(f32[32,32,128]{2,1,0:T(8,128)} %get-tuple-element.39), channel_id=1, source_target_pairs={{0,1},{1,2},{2,3},{3,4},{4,5},{5,6},{6,7},{7,8},{8,9},{9,10},{10,1... | collective-permute-start | bytes 1572872 | tf_op jit(solution)/shard_map/ppermute | solution.py:238
  41.2 1.0 %copy-start.5 = (f32[66,32,128]{2,1,0:T(8,128)}, f32[66,32,128]{2,1,0:T(8,128)S(1)}, u32[]{:S(2)}) copy-start(f32[66,32,128]{2,1,0:T(8,128)S(1)} %get-tuple-element.36.table_ref) | copy-start | bytes 3244036
  42.3 1.0 copy-start.7
  43.2 44.2 %collective-permute-start = (f32[32,32,128]{2,1,0:T(8,128)}, f32[32,32,128]{2,1,0:T(8,128)}, u32[]{:S(2)}, u32[]{:S(2)}) collective-permute-start(f32[32,32,128]{2,1,0:T(8,128)} %get-tuple-element.37), channel_id=1, source_target_pairs={{0,1},{1,2},{2,3},{3,4},{4,5},{5,6},{6,7},{7,8},{8,9},{9,10},{10,1... | collective-permute-start | bytes 1572872 | tf_op jit(solution)/shard_map/ppermute | solution.py:238
  75.5 1.2 %copy-start.14 = (f32[64,32,128]{2,1,0:T(8,128)S(1)}, f32[64,32,128]{2,1,0:T(8,128)}, u32[]{:S(2)}) copy-start(f32[64,32,128]{2,1,0:T(8,128)} %copy-done.13) | copy-start | bytes 3145732
  79.8 1.2 %copy-start.12 = (f32[64,32,128]{2,1,0:T(8,128)S(1)}, f32[64,32,128]{2,1,0:T(8,128)}, u32[]{:S(2)}) copy-start(f32[64,32,128]{2,1,0:T(8,128)} %copy-done.11) | copy-start | bytes 3145732
  81.0 3.2 %copy-start.10 = (f32[64,32,128]{2,1,0:T(8,128)S(1)}, f32[64,32,128]{2,1,0:T(8,128)}, u32[]{:S(2)}) copy-start(f32[64,32,128]{2,1,0:T(8,128)} %copy-done.9) | copy-start | bytes 3145732
  84.2 3.3 %copy-start.6 = (f32[66,32,128]{2,1,0:T(8,128)S(1)}, f32[66,32,128]{2,1,0:T(8,128)}, u32[]{:S(2)}) copy-start(f32[66,32,128]{2,1,0:T(8,128)} %copy-done.5) | copy-start | bytes 3244036
  84.2 3.3 %copy-start.8 = (f32[64,32,128]{2,1,0:T(8,128)S(1)}, f32[64,32,128]{2,1,0:T(8,128)}, u32[]{:S(2)}) copy-start(f32[64,32,128]{2,1,0:T(8,128)} %copy-done.7) | copy-start | bytes 3145732
Sparse Core Ops, SparseCore 0:
  15.2 59.2 all-gather.1

commit v4 on v2

--- a/solution.py
+++ b/solution.py
@@ -10,8 +10,7 @@
 SPAN = 4096
 LANES = 128
 GROUP = 16
-GRANT = 20 * 2**20
-HEAD_GRANT = 57 * 2**20
+GRANT = 16 * 2**20
 MESH = pl.DeviceIdType.MESH
 F32, BF16, I32 = jnp.float32, jnp.bfloat16, jnp.int32
 
@@ -65,15 +64,11 @@
 
 
 def head_kernel(count, tiles, group, scalars_ref, events_ref, keep_ref, prefix_ref, before_ref, *scratch):
-    held, mine, slots, load_sems, send_sems, recv_sems = scratch
-    streams, cols, rows = held.shape
+    mine, slots, send_sems, recv_sems = scratch
+    streams, cols, rows = events_ref.shape
     width = streams * cols
     me = lax.axis_index("rows")
     barrier = pltpu.get_barrier_semaphore()
-
-    loads = [pltpu.make_async_copy(events_ref.at[s], held.at[s], load_sems.at[s]) for s in range(streams)]
-    for load in loads:
-        load.start()
 
     def greet(j, carry):
         @pl.when(j < me)
@@ -87,11 +82,10 @@
 
     def masked(s, g):
         columns = pl.ds(pl.multiple_of(g * span, span), span)
-        return jnp.where(keep_ref[s : s + 1, columns] != 0, held[s, :, columns], 0.0)
+        return jnp.where(keep_ref[s : s + 1, columns] != 0, events_ref[s, :, columns], 0.0)
 
     totals = []
     for s in range(streams):
-        loads[s].wait()
 
         def add(g, total, s=s):
             values = masked(s, g)
@@ -100,7 +94,7 @@
                 parts = [parts[i] + parts[i + 1] for i in range(0, len(parts), 2)]
             return total + parts[0]
 
-        totals.append(lax.fori_loop(0, tiles // group, add, jnp.zeros((cols, LANES), F32)))
+        totals.append(lax.fori_loop(0, tiles // group, add, jnp.zeros((cols, LANES), F32), unroll=True))
     sums = lax.dot_general(
         jnp.ones((8, LANES), F32),
         jnp.concatenate(totals, axis=0),
@@ -257,7 +251,7 @@
     smem = pl.BlockSpec(memory_space=pltpu.SMEM)
     vmem = pl.BlockSpec(memory_space=pltpu.VMEM)
     anywhere = pl.BlockSpec(memory_space=pl.ANY)
-    cost = pl.CostEstimate(flops=10**8, bytes_accessed=8 * 2**20, transcendentals=0)
+    cost = pl.CostEstimate(flops=10**9, bytes_accessed=8 * 2**20, transcendentals=0)
     params = pltpu.CompilerParams(vmem_limit_bytes=GRANT)
 
     rank, slot, scalars = pl.pallas_call(
@@ -268,27 +262,26 @@
             jax.ShapeDtypeStruct((8, everything), I32),
         ),
         scratch_shapes=[pltpu.VMEM((everything, LANES), I32)],
+        cost_estimate=cost,
         compiler_params=params,
         name="index",
     )(keep)
 
     prefix, before = pl.pallas_call(
         functools.partial(head_kernel, count, tiles, group),
-        in_specs=[smem, anywhere, vmem],
+        in_specs=[smem, vmem, vmem],
         out_specs=[vmem, vmem],
         out_shape=[
             jax.ShapeDtypeStruct((everything, cols, LANES), F32),
             jax.ShapeDtypeStruct((8, width), F32),
         ],
         scratch_shapes=[
-            pltpu.VMEM((streams, cols, rows), F32),
             pltpu.VMEM((8, width), F32),
             pltpu.VMEM((count, 8, width), F32),
-            pltpu.SemaphoreType.DMA((streams,)),
             pltpu.SemaphoreType.DMA((count,)),
             pltpu.SemaphoreType.DMA((count,)),
         ],
-        compiler_params=pltpu.CompilerParams(collective_id=0, has_side_effects=True, vmem_limit_bytes=HEAD_GRANT),
+        compiler_params=pltpu.CompilerParams(collective_id=0, has_side_effects=True, vmem_limit_bytes=GRANT),
         name="head",
     )(scalars, events, keep)
 

time: 51.5 us -> 48.6 us (0.944)
  Pallas kernels: 30 us -> 27.8 us
  local copies, waits for them, and re-layouts: 3.68 us -> 3.08 us
    pallas_call x1, Pallas kernels: 12.6 us -> 10.4 us  [per_device(): pl.pallas_call(functools.partial(head_kernel, count, tiles, group), in_sp...]
    unnamed x10 -> x4, local copies, waits for them, and re-layouts: 3.68 us -> 3.08 us
  transfers between devices with their start and end apart: 4 -> 4, of which waited for: 3 -> 3; matrix products, arithmetic and copies ran while one was open for 0% -> 0% of each run, Pallas kernels for 24% -> 26%
where the time goes in v4:
time: 48.6 us; the launch traced here: 48.3 us
  Pallas kernels  27.8 us (57%)
  starting transfers between devices  10.1 us (21%)
  waiting for transfers between devices  6.63 us (14%)
  local copies, waits for them, and re-layouts  3.08 us (6%)
  between operations  0.75 us (2%)
    pallas_call x4, Pallas kernels, per_device(): pl.pallas_call(functools.partial(spread_kernel, s, tiles, group), in_spec...  10.8 us
    pallas_call x1, Pallas kernels, per_device(): pl.pallas_call(functools.partial(head_kernel, count, tiles, group), in_sp...  10.4 us
    ppermute x4, starting transfers between devices, per_device(): lax.ppermute(send, 'rows', [(i, i + 1) for i in range(count - 1)])  10.1 us
    ppermute x4, waiting for transfers between devices, per_device(): lax.ppermute(send, 'rows', [(i, i + 1) for i in range(count - 1)])  6.63 us
    pallas_call x4, Pallas kernels, per_device(): pl.pallas_call(functools.partial(pack_kernel, s, tiles), in_specs=[smem,...  5.68 us
    unnamed x4, local copies, waits for them, and re-layouts  3.08 us
  transfers between devices with their start and end apart: 4, of which 3 were waited for; matrix products, arithmetic and copies ran while one was open for 0% of the time, Pallas kernels for 26%

profile of v4, /device:TPU:8, one launch (start us, length us, event | category | flops | bytes accessed | tf_op | source)
XLA Modules:
  0.0 48.3 jit_solution(449134117070262059)
XLA Ops:
  0.6 0.0 copy-start.1
  0.6 0.9 %copy-done.1 = s32[4,8192]{1,0:T(4,128)S(1)} copy-done((s32[4,8192]{1,0:T(4,128)S(1)}, s32[4,8192]{1,0:T(4,128)}, u32[]{:S(2)}) %copy-start.1) | copy-done | bytes 131096
  1.5 1.0 %index.1 = (s32[256,128]{1,0:T(8,128)S(1)}, s32[256,128]{1,0:T(8,128)S(1)}, s32[8,256]{1,0:T(8,128)S(1)}) custom-call(s32[4,8192]{1,0:T(4,128)S(1)} %copy-done.1), custom_call_target="tpu_custom_call" | custom-call | flops 1000000000 | bytes 8388608 | tf_op jit(solution)/shard_map/index/pallas_call | solution.py:257
  2.5 0.0 copy-start
  2.5 2.2 %copy-done = f32[4,32,8192]{2,1,0:T(8,128)S(1)} copy-done((f32[4,32,8192]{2,1,0:T(8,128)S(1)}, f32[4,32,8192]{2,1,0:T(8,128)}, u32[]{:S(2)}) %copy-start) | copy-done | bytes 4194328
  4.7 10.4 %head.1 = (f32[256,32,128]{2,1,0:T(8,128)S(1)}, f32[8,128]{1,0:T(8,128)S(1)}) custom-call(s32[8,256]{1,0:T(8,128)S(1)} %get-tuple-element.21.scalars_ref, f32[4,32,8192]{2,1,0:T(8,128)S(1)} %copy-done, s32[4,8192]{1,0:T(4,128)S(1)} %copy-done.1), custom_call_target="tpu_custom_call" | custom-call | tf_op jit(solution)/shard_map/head/pallas_call | solution.py:270
  15.1 1.4 %pack0.1 = (f32[66,32,128]{2,1,0:T(8,128)S(1)}, f32[32,32,128]{2,1,0:T(8,128)S(1)}) custom-call(s32[8,256]{1,0:T(8,128)S(1)} %get-tuple-element.21.scalars_ref, f32[256,32,128]{2,1,0:T(8,128)S(1)} %get-tuple-element.24.prefix_ref, s32[256,128]{1,0:T(8,128)S(1)} %get-tuple-element.25.slot_ref), custom_call_target="tpu_custom_call" | custom-call | flops 1000000000 | bytes 8388608 | tf_op jit(solution)/shard_map/pack0/pallas_call | solution.py:290
  16.5 2.0 %collective-permute-start.3 = (f32[32,32,128]{2,1,0:T(8,128)S(1)}, f32[32,32,128]{2,1,0:T(8,128)S(1)}, u32[]{:S(2)}, u32[]{:S(2)}) collective-permute-start(f32[32,32,128]{2,1,0:T(8,128)S(1)} %get-tuple-element.33), channel_id=1, source_target_pairs={{0,1},{1,2},{2,3},{3,4},{4,5},{5,6},{6,7},{7,8},{8,9},{9,10},{10,1... | collective-permute-start | bytes 1572872 | tf_op jit(solution)/shard_map/ppermute | solution.py:302
  18.5 1.4 %pack1.1 = (f32[66,32,128]{2,1,0:T(8,128)S(1)}, f32[32,32,128]{2,1,0:T(8,128)S(1)}) custom-call(s32[8,256]{1,0:T(8,128)S(1)} %get-tuple-element.21.scalars_ref, f32[256,32,128]{2,1,0:T(8,128)S(1)} %get-tuple-element.24.prefix_ref, s32[256,128]{1,0:T(8,128)S(1)} %get-tuple-element.25.slot_ref, f32[66,32,128]{2,1,0:T(8,128)S(1)} %get-tuple-element.26.rest_0_.table_ref), custom_call_target="tpu_custom_call" | custom-call | flops 1000000000 | bytes 8388608 | tf_op jit(solution)/shard_map/pack1/pallas_call | solution.py:290
  20.0 2.5 %collective-permute-start.2 = (f32[32,32,128]{2,1,0:T(8,128)S(1)}, f32[32,32,128]{2,1,0:T(8,128)S(1)}, u32[]{:S(2)}, u32[]{:S(2)}) collective-permute-start(f32[32,32,128]{2,1,0:T(8,128)S(1)} %get-tuple-element.32), channel_id=1, source_target_pairs={{0,1},{1,2},{2,3},{3,4},{4,5},{5,6},{6,7},{7,8},{8,9},{9,10},{10,1... | collective-permute-start | bytes 1572872 | tf_op jit(solution)/shard_map/ppermute | solution.py:302
  22.5 1.4 %pack2.1 = (f32[66,32,128]{2,1,0:T(8,128)S(1)}, f32[32,32,128]{2,1,0:T(8,128)S(1)}) custom-call(s32[8,256]{1,0:T(8,128)S(1)} %get-tuple-element.21.scalars_ref, f32[256,32,128]{2,1,0:T(8,128)S(1)} %get-tuple-element.24.prefix_ref, s32[256,128]{1,0:T(8,128)S(1)} %get-tuple-element.25.slot_ref, f32[66,32,128]{2,1,0:T(8,128)S(1)} %get-tuple-element.27.rest_0_.table_ref), custom_call_target="tpu_custom_call" | custom-call | flops 1000000000 | bytes 8388608 | tf_op jit(solution)/shard_map/pack2/pallas_call | solution.py:290
  23.9 2.1 %collective-permute-start.1 = (f32[32,32,128]{2,1,0:T(8,128)S(1)}, f32[32,32,128]{2,1,0:T(8,128)S(1)}, u32[]{:S(2)}, u32[]{:S(2)}) collective-permute-start(f32[32,32,128]{2,1,0:T(8,128)S(1)} %get-tuple-element.31), channel_id=1, source_target_pairs={{0,1},{1,2},{2,3},{3,4},{4,5},{5,6},{6,7},{7,8},{8,9},{9,10},{10,1... | collective-permute-start | bytes 1572872 | tf_op jit(solution)/shard_map/ppermute | solution.py:302
  26.0 1.4 %pack3.1 = (f32[66,32,128]{2,1,0:T(8,128)S(1)}, f32[32,32,128]{2,1,0:T(8,128)S(1)}) custom-call(s32[8,256]{1,0:T(8,128)S(1)} %get-tuple-element.21.scalars_ref, f32[256,32,128]{2,1,0:T(8,128)S(1)} %get-tuple-element.24.prefix_ref, s32[256,128]{1,0:T(8,128)S(1)} %get-tuple-element.25.slot_ref, f32[66,32,128]{2,1,0:T(8,128)S(1)} %get-tuple-element.28.rest_0_.table_ref), custom_call_target="tpu_custom_call" | custom-call | flops 1000000000 | bytes 8388608 | tf_op jit(solution)/shard_map/pack3/pallas_call | solution.py:290
  27.4 3.5 %collective-permute-start = (f32[32,32,128]{2,1,0:T(8,128)S(1)}, f32[32,32,128]{2,1,0:T(8,128)S(1)}, u32[]{:S(2)}, u32[]{:S(2)}) collective-permute-start(f32[32,32,128]{2,1,0:T(8,128)S(1)} %get-tuple-element.30), channel_id=1, source_target_pairs={{0,1},{1,2},{2,3},{3,4},{4,5},{5,6},{6,7},{7,8},{8,9},{9,10},{10,1... | collective-permute-start | bytes 1572872 | tf_op jit(solution)/shard_map/ppermute | solution.py:302
  30.9 0.0 collective-permute-done.3.tail_ref
  30.9 2.7 %spread0.1 = (f32[4,32,8192]{2,1,0:T(8,128)}, f32[4,32,8192]{2,1,0:T(8,128)}) custom-call(s32[8,256]{1,0:T(8,128)S(1)} %get-tuple-element.21.scalars_ref, f32[8,128]{1,0:T(8,128)S(1)} %get-tuple-element.22.before_ref, s32[256,128]{1,0:T(8,128)S(1)} %get-tuple-element.23.rank_ref, f32[256,32,128]{2,1,0:T(8,128)S(1)} %get-tuple-element.24.prefix_ref, ...), custom_call_target="tpu_custom_call" | custom-call | flops 1000000000 | bytes 8388608 | tf_op jit(solution)/shard_map/spread0/pallas_call | solution.py:307
  33.6 0.8 %collective-permute-done.2.tail_ref = f32[32,32,128]{2,1,0:T(8,128)S(1)} collective-permute-done((f32[32,32,128]{2,1,0:T(8,128)S(1)}, f32[32,32,128]{2,1,0:T(8,128)S(1)}, u32[]{:S(2)}, u32[]{:S(2)}) %collective-permute-start.2) | collective-permute-done | bytes 524320 | tf_op jit(solution)/shard_map/ppermute | solution.py:302
  34.4 2.7 %spread1.1 = (f32[4,32,8192]{2,1,0:T(8,128)}, f32[4,32,8192]{2,1,0:T(8,128)}) custom-call(s32[8,256]{1,0:T(8,128)S(1)} %get-tuple-element.21.scalars_ref, f32[8,128]{1,0:T(8,128)S(1)} %get-tuple-element.22.before_ref, s32[256,128]{1,0:T(8,128)S(1)} %get-tuple-element.23.rank_ref, ...), custom_call_target="tpu_custom_call", output_to_operand_aliasing={{0}: (6, {}), {1}: (7, {})} | custom-call | flops 1000000000 | bytes 8388608 | tf_op jit(solution)/shard_map/spread1/pallas_call | solution.py:307
  37.1 2.9 %collective-permute-done.1.tail_ref = f32[32,32,128]{2,1,0:T(8,128)S(1)} collective-permute-done((f32[32,32,128]{2,1,0:T(8,128)S(1)}, f32[32,32,128]{2,1,0:T(8,128)S(1)}, u32[]{:S(2)}, u32[]{:S(2)}) %collective-permute-start.1) | collective-permute-done | bytes 524320 | tf_op jit(solution)/shard_map/ppermute | solution.py:302
  40.0 2.7 %spread2.1 = (f32[4,32,8192]{2,1,0:T(8,128)}, f32[4,32,8192]{2,1,0:T(8,128)}) custom-call(s32[8,256]{1,0:T(8,128)S(1)} %get-tuple-element.21.scalars_ref, f32[8,128]{1,0:T(8,128)S(1)} %get-tuple-element.22.before_ref, s32[256,128]{1,0:T(8,128)S(1)} %get-tuple-element.23.rank_ref, ...), custom_call_target="tpu_custom_call", output_to_operand_aliasing={{0}: (6, {}), {1}: (7, {})} | custom-call | flops 1000000000 | bytes 8388608 | tf_op jit(solution)/shard_map/spread2/pallas_call | solution.py:307
  42.7 2.9 %collective-permute-done.tail_ref = f32[32,32,128]{2,1,0:T(8,128)S(1)} collective-permute-done((f32[32,32,128]{2,1,0:T(8,128)S(1)}, f32[32,32,128]{2,1,0:T(8,128)S(1)}, u32[]{:S(2)}, u32[]{:S(2)}) %collective-permute-start) | collective-permute-done | bytes 524320 | tf_op jit(solution)/shard_map/ppermute | solution.py:302
  45.7 2.7 %spread3.1 = (f32[4,32,8192]{2,1,0:T(8,128)}, f32[4,32,8192]{2,1,0:T(8,128)}) custom-call(s32[8,256]{1,0:T(8,128)S(1)} %get-tuple-element.21.scalars_ref, f32[8,128]{1,0:T(8,128)S(1)} %get-tuple-element.22.before_ref, s32[256,128]{1,0:T(8,128)S(1)} %get-tuple-element.23.rank_ref, ...), custom_call_target="tpu_custom_call", output_to_operand_aliasing={{0}: (6, {}), {1}: (7, {})} | custom-call | flops 1000000000 | bytes 8388608 | tf_op jit(solution)/shard_map/spread3/pallas_call | solution.py:307
Async XLA Ops:
  0.6 0.9 %copy-start.1 = (s32[4,8192]{1,0:T(4,128)S(1)}, s32[4,8192]{1,0:T(4,128)}, u32[]{:S(2)}) copy-start(s32[4,8192]{1,0:T(4,128)} %keep_ref.3) | copy-start | bytes 393220
  2.5 2.2 %copy-start = (f32[4,32,8192]{2,1,0:T(8,128)S(1)}, f32[4,32,8192]{2,1,0:T(8,128)}, u32[]{:S(2)}) copy-start(f32[4,32,8192]{2,1,0:T(8,128)} %events_ref.1) | copy-start | bytes 12582916
  16.5 14.4 %collective-permute-start.3 = (f32[32,32,128]{2,1,0:T(8,128)S(1)}, f32[32,32,128]{2,1,0:T(8,128)S(1)}, u32[]{:S(2)}, u32[]{:S(2)}) collective-permute-start(f32[32,32,128]{2,1,0:T(8,128)S(1)} %get-tuple-element.33), channel_id=1, source_target_pairs={{0,1},{1,2},{2,3},{3,4},{4,5},{5,6},{6,7},{7,8},{8,9},{9,10},{10,1... | collective-permute-start | bytes 1572872 | tf_op jit(solution)/shard_map/ppermute | solution.py:302
  20.0 14.5 %collective-permute-start.2 = (f32[32,32,128]{2,1,0:T(8,128)S(1)}, f32[32,32,128]{2,1,0:T(8,128)S(1)}, u32[]{:S(2)}, u32[]{:S(2)}) collective-permute-start(f32[32,32,128]{2,1,0:T(8,128)S(1)} %get-tuple-element.32), channel_id=1, source_target_pairs={{0,1},{1,2},{2,3},{3,4},{4,5},{5,6},{6,7},{7,8},{8,9},{9,10},{10,1... | collective-permute-start | bytes 1572872 | tf_op jit(solution)/shard_map/ppermute | solution.py:302
  23.9 16.1 %collective-permute-start.1 = (f32[32,32,128]{2,1,0:T(8,128)S(1)}, f32[32,32,128]{2,1,0:T(8,128)S(1)}, u32[]{:S(2)}, u32[]{:S(2)}) collective-permute-start(f32[32,32,128]{2,1,0:T(8,128)S(1)} %get-tuple-element.31), channel_id=1, source_target_pairs={{0,1},{1,2},{2,3},{3,4},{4,5},{5,6},{6,7},{7,8},{8,9},{9,10},{10,1... | collective-permute-start | bytes 1572872 | tf_op jit(solution)/shard_map/ppermute | solution.py:302
  27.4 18.3 %collective-permute-start = (f32[32,32,128]{2,1,0:T(8,128)S(1)}, f32[32,32,128]{2,1,0:T(8,128)S(1)}, u32[]{:S(2)}, u32[]{:S(2)}) collective-permute-start(f32[32,32,128]{2,1,0:T(8,128)S(1)} %get-tuple-element.30), channel_id=1, source_target_pairs={{0,1},{1,2},{2,3},{3,4},{4,5},{5,6},{6,7},{7,8},{8,9},{9,10},{10,1... | collective-permute-start | bytes 1572872 | tf_op jit(solution)/shard_map/ppermute | solution.py:302
